TPU v7x, 768 devices: a whole 4x8x12 slice. The times are simulated.
768 devices in a mesh: dom: 96 (over y_hi, z, core), sub: 8 (over x, y_lo).
Axes of the slice: x: 4, y: 8 (y_hi: 4, y_lo: 2; y = y_hi * 2 + y_lo), z: 12, core: 2. Of those that a mesh axis runs over, the one named last changes fastest.
Arguments:
- state: float32 [9, 10, 196608], P(None, None, ('dom', 'sub')), may hold values from -6 to 6
- geometry: float32 [3, 3, 196608], P(None, None, ('dom', 'sub')), may hold values from -4 to 4
- face_scale: float32 [4, 196608], P(None, ('dom', 'sub')), may hold values from 0.2 to 1
- material: int32 [196608], P(('dom', 'sub')), may hold values from 0 to 2
- cluster: int32 [196608], P(('dom', 'sub')), may hold values from 0 to 1, as said below
- neighbours: int32 [4, 196608], P(None, ('dom', 'sub')), may hold values from 0 to 1023, as said below
- orientation: int32 [4, 196608], P(None, ('dom', 'sub')), may hold values from 0 to 11
- stiffness: float32 [3, 10, 10], replicated, may hold values from -2 to 2
- jacobians: float32 [3, 3, 9, 9], replicated, may hold values from -2 to 2
- flux_local: float32 [4, 10, 10], replicated, may hold values from -2 to 2
- flux_neigh: float32 [12, 10, 10], replicated, may hold values from -2 to 2
- flux_plus: float32 [3, 9, 9], replicated, may hold values from -2 to 2
- flux_minus: float32 [3, 9, 9], replicated, may hold values from -2 to 2
Outputs:
- final_state: float32 [9, 10, 196608], P(None, None, ('dom', 'sub'))
Inputs may be any that keep to these rules, and one draw needn't show every extreme that they name: Face neighbours are numbered in the table of the face's own partition, as the first step says. `cluster`: 0 marks a fine tetrahedron, 1 a coarse one.
All inputs are finite; a program needn't handle non-finite values.
Results may differ from a plain program's by a relative error of at most 0.0003.
Values sent between devices are 32-bit elements; how exact they have to be, the bound alone decides.
No kernel may reach another device: no remote copies, remote signals or barrier semaphores. Data moves between devices by JAX's collectives and lax.ppermute only.
A program may use at most 64 MiB of HBM per device.

v0:
```python
import jax
import jax.numpy as jnp
from jax import lax
from jax.sharding import PartitionSpec as P

COPY_DEV = 128
SUB_COPY = 64


step_length = 0.2


def laid_out(parts, dim):
    parts = jnp.moveaxis(parts, 0, dim)
    shape = parts.shape
    return parts.reshape(*shape[:dim], shape[dim] * shape[dim + 1], *shape[dim + 2 :])


def sent_to_all(value, axis):
    devices = lax.axis_size(axis)
    return lax.all_to_all(
        jnp.broadcast_to(value[None], (devices, *value.shape)), axis, 0, 0, tiled=True
    )


def gathered_copies(value, axis, dim):
    return laid_out(sent_to_all(value, axis), dim)


def from_behind(block, axis, distance):
    devices = range(lax.axis_size(axis))
    route = [((i - distance) % len(devices), i) for i in devices]
    return lax.ppermute(block, axis, route)


def per_element(matrix, values):
    total = matrix[:, 0][:, None, :] * values[0][None, :, :]
    for inner in range(1, matrix.shape[1]):
        total = total + matrix[:, inner][:, None, :] * values[inner][None, :, :]
    return total


def per_element_basis(matrix, values):
    total = matrix[None, :, 0, :] * values[:, 0][:, None, :]
    for inner in range(1, matrix.shape[1]):
        total = total + matrix[None, :, inner, :] * values[:, inner][:, None, :]
    return total


def apply_star(values, stiffness, geometry, element_jac, transpose):
    pattern = "ba,vbe->vae" if transpose else "ab,vbe->vae"
    mapped = [
        jnp.einsum(pattern, stiffness[direction], values, precision=lax.Precision.HIGHEST)
        for direction in range(3)
    ]
    summed = jnp.zeros_like(values)
    for column in range(3):
        mixture = (
            mapped[0] * geometry[0, column]
            + mapped[1] * geometry[1, column]
            + mapped[2] * geometry[2, column]
        )
        summed = summed + per_element(element_jac[column], mixture)
    return summed


def predict(values, stiffness, geometry, element_jac, coarse, shifted):
    first = -apply_star(values, stiffness, geometry, element_jac, False)
    second = -apply_star(first, stiffness, geometry, element_jac, False)
    if shifted:
        values = values + coarse * (step_length * first + 0.5 * step_length**2 * second)
        first = first + coarse * (step_length * second)
    return step_length * values + step_length**2 / 2 * first + step_length**3 / 6 * second


def update(
    own,
    neighbour_parts,
    face_scale,
    stiffness,
    geometry,
    element_jac,
    element_plus,
    element_minus,
    face_neigh,
    flux_local,
):
    result = apply_star(own, stiffness, geometry, element_jac, True)
    plus = per_element(element_plus, own)
    for face in range(4):
        minus = per_element(element_minus, neighbour_parts[face])
        across = jnp.einsum("ab,vbe->vae", flux_local[face], plus, precision=lax.Precision.HIGHEST)
        across = across + per_element_basis(face_neigh[face], minus)
        result = result - face_scale[face] * across
    return result


def element_tables(material, orientation, jacobians, flux_plus, flux_minus, flux_neigh):
    medium_mask = (material[None, :] == jnp.arange(3, dtype=jnp.int32)[:, None]).astype(jnp.float32)
    element_jac = jnp.einsum(
        "mcvw,me->cvwe", jacobians, medium_mask, precision=lax.Precision.HIGHEST
    )
    element_plus = jnp.einsum(
        "mvw,me->vwe", flux_plus, medium_mask, precision=lax.Precision.HIGHEST
    )
    element_minus = jnp.einsum(
        "mvw,me->vwe", flux_minus, medium_mask, precision=lax.Precision.HIGHEST
    )
    turns = jnp.arange(12, dtype=jnp.int32)[:, None]
    face_neigh = [
        jnp.einsum(
            "tab,te->abe",
            flux_neigh,
            (orientation[face][None, :] == turns).astype(jnp.float32),
            precision=lax.Precision.HIGHEST,
        )
        for face in range(4)
    ]
    return (element_jac, element_plus, element_minus, face_neigh)


def share(lower, upper):
    from_group = gathered_copies(lower[:, :, :SUB_COPY], "sub", 2)
    from_left = from_behind(upper, "dom", 1)
    from_right = from_behind(lower, "dom", -1)
    return [from_group, from_left, from_right]


def shards(
    state,
    geometry,
    face_scale,
    material,
    cluster,
    neighbours,
    orientation,
    stiffness,
    jacobians,
    flux_local,
    flux_neigh,
    flux_plus,
    flux_minus,
):
    count = state.shape[2]
    element_jac, element_plus, element_minus, face_neigh = element_tables(
        material, orientation, jacobians, flux_plus, flux_minus, flux_neigh
    )
    coarse = cluster.astype(jnp.float32)
    finer = 1.0 - coarse

    def integrate(values, shifted):
        whole = predict(values, stiffness, geometry, element_jac, coarse, shifted)
        outside = share(whole[:, :, :COPY_DEV], whole[:, :, count - COPY_DEV :])
        return (whole, jnp.concatenate([whole] + outside, axis=2))

    def advance(values, shifted):
        integral, table = integrate(values, shifted)
        parts = [jnp.take(table, neighbours[face], axis=2) for face in range(4)]
        return update(
            integral,
            parts,
            face_scale,
            stiffness,
            geometry,
            element_jac,
            element_plus,
            element_minus,
            face_neigh,
            flux_local,
        )

    first_change = advance(state, False)
    middle = state + finer * first_change
    second_change = advance(middle, True)
    state = middle + finer * second_change + coarse * (first_change + second_change)
    return state


def solution(mesh):
    placed = (
        P(None, None, ("dom", "sub")),
        P(None, None, ("dom", "sub")),
        P(None, ("dom", "sub")),
        P(("dom", "sub")),
        P(("dom", "sub")),
        P(None, ("dom", "sub")),
        P(None, ("dom", "sub")),
        P(),
        P(),
        P(),
        P(),
        P(),
        P(),
    )
    return jax.shard_map(
        shards, mesh=mesh, in_specs=placed, out_specs=P(None, None, ("dom", "sub")), check_vma=False
    )
```

profile of v0, /device:TPU:8, one launch (start us, length us, event | category | flops | bytes accessed | tf_op | source)
XLA Modules:
  0.0 185.1 jit_solution(4800816595213517526)
XLA Ops:
  0.0 0.9 fusion.83
  0.9 1.2 fusion.38
  2.1 1.2 fusion.44
  3.2 0.9 fusion.84
  4.2 1.2 convolution_bitcast_fusion
  7.9 1.0 multiply_add_fusion.13
  8.9 16.8 %collective-permute-start.1 = (f32[9,10,128]{2,1,0:T(8,128)S(1)}, f32[9,10,128]{2,1,0:T(8,128)S(1)}, u32[]{:S(2)}, u32[]{:S(2)}) collective-permute-start(f32[9,10,128]{2,1,0:T(8,128)S(1)} %get-tuple-element.348), channel_id=1, source_target_pairs={{8,0},{16,8},{24,16},{32,24},{40,32},{48,40},{56,48},{64,56},{72,6... | collective-permute-start | bytes 138248 | tf_op jit(solution)/shard_map/ppermute | solution.py:33
  25.8 1.9 %collective-permute-start = (f32[9,10,128]{2,1,0:T(8,128)S(1)}, f32[9,10,128]{2,1,0:T(8,128)S(1)}, u32[]{:S(2)}, u32[]{:S(2)}) collective-permute-start(f32[9,10,128]{2,1,0:T(8,128)S(1)} %get-tuple-element.347), channel_id=1, source_target_pairs={{760,0},{0,8},{8,16},{16,24},{24,32},{32,40},{40,48},{48,56},{56,6... | collective-permute-start | bytes 138248 | tf_op jit(solution)/shard_map/ppermute | solution.py:33
  27.8 0.9 reshape.169
  28.7 5.8 %all-to-all-start = ((f32[8,1,5760]{2,1,0:T(1,128)}), f32[8,1,5760]{2,1,0:T(1,128)S(1)}, u32[]{:S(2)}, u32[]{:S(2)}) async-start(f32[8,1,5760]{2,1,0:T(1,128)} %reshape.169), calls=%async_computation | async-start | bytes 368640 | tf_op jit(solution)/shard_map/all_to_all | solution.py:21
  57.5 1.0 reduce
  59.0 6.1 %copy.140 = f32[9,10,1024]{1,0,2:T(8,128)} copy(f32[9,10,1024]{2,1,0:T(8,128)S(1)} %pad_maximum_fusion) | data formatting | bytes 737280 | tf_op jit(solution)/shard_map/concatenate | solution.py:154
  65.1 4.1 %gather_fusion.3 = f32[256,9,10]{2,1,0:T(8,128)S(1)} fusion(f32[9,10,1024]{1,0,2:T(8,128)} %copy.140, s32[1024]{0:T(1024)S(1)} %pad_clamp_fusion), kind=kCustom, calls=%fused_computation.3.clone | custom fusion | bytes 185344 | tf_op jit(solution)/shard_map/jit(_take)/gather | solution.py:158
  72.0 4.1 %gather_fusion.2 = f32[256,9,10]{2,1,0:T(8,128)S(1)} fusion(f32[9,10,1024]{1,0,2:T(8,128)} %copy.140, s32[1024]{0:T(1024)S(1)} %pad_clamp_fusion.1), kind=kCustom, calls=%fused_computation.2.clone | custom fusion | bytes 185344 | tf_op jit(solution)/shard_map/jit(_take)/gather | solution.py:158
  78.8 4.3 %gather_fusion.1 = f32[256,9,10]{2,1,0:T(8,128)S(1)} fusion(f32[9,10,1024]{1,0,2:T(8,128)} %copy.140, s32[1024]{0:T(1024)} %pad_clamp_fusion.2), kind=kCustom, calls=%fused_computation.1.clone | custom fusion | bytes 185344 | tf_op jit(solution)/shard_map/jit(_take)/gather | solution.py:158
  85.8 4.1 %gather_fusion = f32[256,9,10]{2,1,0:T(8,128)S(1)} fusion(f32[9,10,1024]{1,0,2:T(8,128)} %copy.140, s32[1024]{0:T(1024)S(1)} %pad_clamp_fusion.3), kind=kCustom, calls=%fused_computation.clone | custom fusion | bytes 185344 | tf_op jit(solution)/shard_map/jit(_take)/gather | solution.py:158
  92.5 1.2 fusion.15
  93.7 1.2 fusion.14
  95.0 1.2 fusion.13
  96.6 2.6 %multiply_add_fusion.11 = (f32[9,10,256]{2,1,0:T(8,128)S(1)}, f32[9,10,256]{2,1,0:T(8,128)}) fusion(f32[9,10,256]{2,1,0:T(8,128)S(1)} %copy-done.2, f32[256]{0:T(256)} %get-tuple-element.477, f32[9,10,256]{2,1,0:T(8,128)S(1)} %fusion.15, f32[9,10,256]{2,1,0:T(8,128)S(1)} %fusion.14, f32[9,10,256]{2,1,0:T(8,128)S(1)} %fusion.13, ...), kind=kOutput, calls=%fused_computation.81 | convolution fusion | flops 4608000 | bytes 1367440 | tf_op jit(solution)/shard_map/ab,vbe->vae/dot_general | solution.py:92
  101.8 1.3 multiply_add_fusion.10
  103.8 7.3 %collective-permute-start.3 = (f32[9,10,128]{2,1,0:T(8,128)S(1)}, f32[9,10,128]{2,1,0:T(8,128)S(1)}, u32[]{:S(2)}, u32[]{:S(2)}) collective-permute-start(f32[9,10,128]{2,1,0:T(8,128)S(1)} %get-tuple-element.247), channel_id=1, source_target_pairs={{8,0},{16,8},{24,16},{32,24},{40,32},{48,40},{56,48},{64,56},{72,6... | collective-permute-start | bytes 138248 | tf_op jit(solution)/shard_map/ppermute | solution.py:33
  111.1 1.9 %collective-permute-start.2 = (f32[9,10,128]{2,1,0:T(8,128)S(1)}, f32[9,10,128]{2,1,0:T(8,128)S(1)}, u32[]{:S(2)}, u32[]{:S(2)}) collective-permute-start(f32[9,10,128]{2,1,0:T(8,128)S(1)} %get-tuple-element.246), channel_id=1, source_target_pairs={{760,0},{0,8},{8,16},{16,24},{24,32},{32,40},{40,48},{48,56},{56,6... | collective-permute-start | bytes 138248 | tf_op jit(solution)/shard_map/ppermute | solution.py:33
  113.1 0.9 reshape.171
  114.0 5.7 %all-to-all-start.1 = ((f32[8,1,5760]{2,1,0:T(1,128)}), f32[8,1,5760]{2,1,0:T(1,128)S(1)}, u32[]{:S(2)}, u32[]{:S(2)}) async-start(f32[8,1,5760]{2,1,0:T(1,128)} %reshape.171), calls=%async_computation.1 | async-start | bytes 368640 | tf_op jit(solution)/shard_map/all_to_all | solution.py:21
  122.8 2.6 %all-to-all-done.1 = f32[8,1,5760]{2,1,0:T(1,128)S(1)} async-done(((f32[8,1,5760]{2,1,0:T(1,128)}), f32[8,1,5760]{2,1,0:T(1,128)S(1)}, u32[]{:S(2)}, u32[]{:S(2)}) %all-to-all-start.1) | async-done | bytes 184352 | tf_op jit(solution)/shard_map/all_to_all | solution.py:21
  125.4 1.0 reduce.1
  126.9 6.1 %copy.190 = f32[9,10,1024]{1,0,2:T(8,128)} copy(f32[9,10,1024]{2,1,0:T(8,128)S(1)} %pad_maximum_fusion.1) | data formatting | bytes 737280 | tf_op jit(solution)/shard_map/concatenate | solution.py:154
  133.0 5.6 %gather_fusion.7 = f32[256,9,10]{2,1,0:T(8,128)} fusion(f32[9,10,1024]{1,0,2:T(8,128)} %copy.190, s32[1024]{0:T(1024)} %copy-done.128), kind=kCustom, calls=%fused_computation.7.clone | custom fusion | bytes 185344 | tf_op jit(solution)/shard_map/jit(_take)/gather | solution.py:158
  138.6 5.6 %gather_fusion.6 = f32[256,9,10]{2,1,0:T(8,128)} fusion(f32[9,10,1024]{1,0,2:T(8,128)} %copy.190, s32[1024]{0:T(1024)} %copy-done.129), kind=kCustom, calls=%fused_computation.6.clone | custom fusion | bytes 185344 | tf_op jit(solution)/shard_map/jit(_take)/gather | solution.py:158
  144.2 5.6 %gather_fusion.5 = f32[256,9,10]{2,1,0:T(8,128)} fusion(f32[9,10,1024]{1,0,2:T(8,128)} %copy.190, s32[1024]{0:T(1024)} %pad_clamp_fusion.2), kind=kCustom, calls=%fused_computation.5.clone | custom fusion | bytes 185344 | tf_op jit(solution)/shard_map/jit(_take)/gather | solution.py:158
  149.8 4.3 %gather_fusion.4 = f32[256,9,10]{2,1,0:T(8,128)S(1)} fusion(f32[9,10,1024]{1,0,2:T(8,128)} %copy.190, s32[1024]{0:T(1024)} %copy-done.130), kind=kCustom, calls=%fused_computation.4.clone | custom fusion | bytes 185344 | tf_op jit(solution)/shard_map/jit(_take)/gather | solution.py:158
  154.1 1.9 %select_bitcast_fusion = f32[9,10,256]{1,0,2:T(8,128)S(1)} fusion(f32[256,9,10]{2,1,0:T(8,128)} %gather_fusion.7, pred[256]{0:T(512)(128)(4,1)S(1)} %copy-done.140), kind=kLoop, calls=%fused_computation.8 | loop fusion | flops 23040 | bytes 184576 | tf_op jit(solution)/shard_map/jit(_take)/select_n | solution.py:158
  156.0 1.3 fusion.66
  157.4 1.0 copy.229
  159.6 0.8 multiply_add_fusion
  161.2 1.9 %select_bitcast_fusion.1 = f32[9,10,256]{1,0,2:T(8,128)S(1)} fusion(f32[256,9,10]{2,1,0:T(8,128)} %gather_fusion.6, pred[256]{0:T(512)(128)(4,1)} %compare_and_fusion.1), kind=kLoop, calls=%fused_computation.9 | loop fusion | flops 23040 | bytes 184576 | tf_op jit(solution)/shard_map/jit(_take)/select_n | solution.py:158
  163.1 1.3 fusion.65
  164.4 1.0 copy.219
  166.7 0.8 multiply_add_fusion.1
  168.2 1.9 %select_bitcast_fusion.2 = f32[9,10,256]{1,0,2:T(8,128)S(1)} fusion(f32[256,9,10]{2,1,0:T(8,128)} %gather_fusion.5, pred[256]{0:T(512)(128)(4,1)} %compare_and_fusion.2), kind=kLoop, calls=%fused_computation.10 | loop fusion | flops 23040 | bytes 184576 | tf_op jit(solution)/shard_map/jit(_take)/select_n | solution.py:158
  170.2 1.3 fusion.64
  171.5 1.0 copy.209
  175.2 1.0 select_bitcast_fusion.3
  178.3 1.2 fusion.23
  179.5 1.3 fusion.22
  180.8 1.2 fusion.21
  182.4 2.6 %multiply_add_fusion.8 = f32[9,10,256]{2,1,0:T(8,128)} fusion(f32[9,10,256]{2,1,0:T(8,128)} %get-tuple-element.479, f32[9,10,256]{2,1,0:T(8,128)S(1)} %get-tuple-element.478, f32[9,10,256]{2,1,0:T(8,128)S(1)} %fusion.23, f32[9,10,256]{2,1,0:T(8,128)S(1)} %fusion.22, f32[9,10,256]{2,1,0:T(8,128)S(1)} %fusion.21, f32[9,10,256]{2,1,0:T(8,128)S(1)} %copy-done.51, ...), kind=kOutput, calls=%fused_computation.68 | convolution fusion | flops 4677120 | bytes 1368464 | tf_op jit(solution)/shard_map/ab,vbe->vae/dot_general | solution.py:92
  (521 shorter events, 50.6 us)
Async XLA Ops:
  0.0 38.1 %copy-start = (f32[12,10,10]{2,0,1:T(8,128)S(1)}, f32[12,10,10]{2,0,1:T(8,128)}, u32[]{:S(2)}) copy-start(f32[12,10,10]{2,0,1:T(8,128)} %param.25) | copy-start | bytes 14404
  4.1 37.3 %copy-start.52 = (f32[1,1,256]{2,1,0:T(1,128)}, f32[1,1,256]{2,1,0:T(1,128)S(1)}, u32[]{:S(2)}) copy-start(f32[1,1,256]{2,1,0:T(1,128)S(1)} %get-tuple-element.457) | copy-start | bytes 3076
  4.1 37.3 %copy-start.54 = (f32[1,1,256]{2,1,0:T(1,128)}, f32[1,1,256]{2,1,0:T(1,128)S(1)}, u32[]{:S(2)}) copy-start(f32[1,1,256]{2,1,0:T(1,128)S(1)} %get-tuple-element.458) | copy-start | bytes 3076
  4.1 37.3 %copy-start.56 = (f32[1,1,256]{2,1,0:T(1,128)}, f32[1,1,256]{2,1,0:T(1,128)S(1)}, u32[]{:S(2)}) copy-start(f32[1,1,256]{2,1,0:T(1,128)S(1)} %get-tuple-element.459) | copy-start | bytes 3076
  4.1 37.3 %copy-start.58 = (f32[1,1,256]{2,1,0:T(1,128)}, f32[1,1,256]{2,1,0:T(1,128)S(1)}, u32[]{:S(2)}) copy-start(f32[1,1,256]{2,1,0:T(1,128)S(1)} %get-tuple-element.460) | copy-start | bytes 3076
  4.1 37.3 %copy-start.60 = (f32[1,1,256]{2,1,0:T(1,128)}, f32[1,1,256]{2,1,0:T(1,128)S(1)}, u32[]{:S(2)}) copy-start(f32[1,1,256]{2,1,0:T(1,128)S(1)} %get-tuple-element.461) | copy-start | bytes 3076
  4.2 37.3 %copy-start.62 = (f32[1,1,256]{2,1,0:T(1,128)}, f32[1,1,256]{2,1,0:T(1,128)S(1)}, u32[]{:S(2)}) copy-start(f32[1,1,256]{2,1,0:T(1,128)S(1)} %get-tuple-element.462) | copy-start | bytes 3076
  4.2 37.3 %copy-start.64 = (f32[1,1,256]{2,1,0:T(1,128)}, f32[1,1,256]{2,1,0:T(1,128)S(1)}, u32[]{:S(2)}) copy-start(f32[1,1,256]{2,1,0:T(1,128)S(1)} %get-tuple-element.463) | copy-start | bytes 3076
  5.7 95.8 %copy-start.3 = (f32[9,1,256]{2,0,1:T(8,128)}, f32[9,1,256]{2,0,1:T(8,128)S(1)}, u32[]{:S(2)}) copy-start(f32[9,1,256]{2,0,1:T(8,128)S(1)} %copy.481) | copy-start | bytes 27652
  5.8 95.8 %copy-start.5 = (f32[9,1,256]{2,0,1:T(8,128)}, f32[9,1,256]{2,0,1:T(8,128)S(1)}, u32[]{:S(2)}) copy-start(f32[9,1,256]{2,0,1:T(8,128)S(1)} %copy.482) | copy-start | bytes 27652
  5.8 95.8 %copy-start.7 = (f32[9,1,256]{2,0,1:T(8,128)}, f32[9,1,256]{2,0,1:T(8,128)S(1)}, u32[]{:S(2)}) copy-start(f32[9,1,256]{2,0,1:T(8,128)S(1)} %copy.483) | copy-start | bytes 27652
  5.8 95.8 %copy-start.9 = (f32[9,1,256]{2,0,1:T(8,128)}, f32[9,1,256]{2,0,1:T(8,128)S(1)}, u32[]{:S(2)}) copy-start(f32[9,1,256]{2,0,1:T(8,128)S(1)} %copy.484) | copy-start | bytes 27652
  6.2 95.4 %copy-start.11 = (f32[9,1,256]{2,0,1:T(8,128)}, f32[9,1,256]{2,0,1:T(8,128)S(1)}, u32[]{:S(2)}) copy-start(f32[9,1,256]{2,0,1:T(8,128)S(1)} %copy.485) | copy-start | bytes 27652
  6.2 95.4 %copy-start.13 = (f32[9,1,256]{2,0,1:T(8,128)}, f32[9,1,256]{2,0,1:T(8,128)S(1)}, u32[]{:S(2)}) copy-start(f32[9,1,256]{2,0,1:T(8,128)S(1)} %copy.486) | copy-start | bytes 27652
  6.2 95.4 %copy-start.15 = (f32[9,1,256]{2,0,1:T(8,128)}, f32[9,1,256]{2,0,1:T(8,128)S(1)}, u32[]{:S(2)}) copy-start(f32[9,1,256]{2,0,1:T(8,128)S(1)} %copy.487) | copy-start | bytes 27652
  6.2 95.4 %copy-start.17 = (f32[9,1,256]{2,0,1:T(8,128)}, f32[9,1,256]{2,0,1:T(8,128)S(1)}, u32[]{:S(2)}) copy-start(f32[9,1,256]{2,0,1:T(8,128)S(1)} %copy.488) | copy-start | bytes 27652
  6.3 95.3 %copy-start.19 = (f32[9,1,256]{2,0,1:T(8,128)}, f32[9,1,256]{2,0,1:T(8,128)S(1)}, u32[]{:S(2)}) copy-start(f32[9,1,256]{2,0,1:T(8,128)S(1)} %copy.489) | copy-start | bytes 27652
  6.3 95.3 %copy-start.21 = (f32[9,1,256]{2,0,1:T(8,128)}, f32[9,1,256]{2,0,1:T(8,128)S(1)}, u32[]{:S(2)}) copy-start(f32[9,1,256]{2,0,1:T(8,128)S(1)} %copy.490) | copy-start | bytes 27652
  6.3 95.3 %copy-start.23 = (f32[9,1,256]{2,0,1:T(8,128)}, f32[9,1,256]{2,0,1:T(8,128)S(1)}, u32[]{:S(2)}) copy-start(f32[9,1,256]{2,0,1:T(8,128)S(1)} %copy.491) | copy-start | bytes 27652
  6.3 95.3 %copy-start.25 = (f32[9,1,256]{2,0,1:T(8,128)}, f32[9,1,256]{2,0,1:T(8,128)S(1)}, u32[]{:S(2)}) copy-start(f32[9,1,256]{2,0,1:T(8,128)S(1)} %copy.492) | copy-start | bytes 27652
  6.3 95.3 %copy-start.27 = (f32[9,1,256]{2,0,1:T(8,128)}, f32[9,1,256]{2,0,1:T(8,128)S(1)}, u32[]{:S(2)}) copy-start(f32[9,1,256]{2,0,1:T(8,128)S(1)} %copy.493) | copy-start | bytes 27652
  6.4 95.3 %copy-start.29 = (f32[9,256]{1,0:T(8,128)}, f32[9,256]{1,0:T(8,128)S(1)}, u32[]{:S(2)}) copy-start(f32[9,256]{1,0:T(8,128)S(1)} %get-tuple-element.498) | copy-start | bytes 27652
  6.4 95.3 %copy-start.31 = (f32[9,256]{1,0:T(8,128)}, f32[9,256]{1,0:T(8,128)S(1)}, u32[]{:S(2)}) copy-start(f32[9,256]{1,0:T(8,128)S(1)} %get-tuple-element.499) | copy-start | bytes 27652
  6.4 95.2 %copy-start.33 = (f32[9,256]{1,0:T(8,128)}, f32[9,256]{1,0:T(8,128)S(1)}, u32[]{:S(2)}) copy-start(f32[9,256]{1,0:T(8,128)S(1)} %get-tuple-element.500) | copy-start | bytes 27652
  6.4 95.2 %copy-start.35 = (f32[9,256]{1,0:T(8,128)}, f32[9,256]{1,0:T(8,128)S(1)}, u32[]{:S(2)}) copy-start(f32[9,256]{1,0:T(8,128)S(1)} %get-tuple-element.501) | copy-start | bytes 27652
  6.5 95.2 %copy-start.37 = (f32[9,256]{1,0:T(8,128)}, f32[9,256]{1,0:T(8,128)S(1)}, u32[]{:S(2)}) copy-start(f32[9,256]{1,0:T(8,128)S(1)} %get-tuple-element.502) | copy-start | bytes 27652
  6.5 95.2 %copy-start.39 = (f32[9,256]{1,0:T(8,128)}, f32[9,256]{1,0:T(8,128)S(1)}, u32[]{:S(2)}) copy-start(f32[9,256]{1,0:T(8,128)S(1)} %get-tuple-element.503) | copy-start | bytes 27652
  6.5 95.2 %copy-start.41 = (f32[9,256]{1,0:T(8,128)}, f32[9,256]{1,0:T(8,128)S(1)}, u32[]{:S(2)}) copy-start(f32[9,256]{1,0:T(8,128)S(1)} %get-tuple-element.504) | copy-start | bytes 27652
  6.5 95.2 %copy-start.43 = (f32[9,256]{1,0:T(8,128)}, f32[9,256]{1,0:T(8,128)S(1)}, u32[]{:S(2)}) copy-start(f32[9,256]{1,0:T(8,128)S(1)} %get-tuple-element.505) | copy-start | bytes 27652
  7.9 26.6 %copy-start.134 = (s32[4,256]{1,0:T(4,128)S(1)}, s32[4,256]{1,0:T(4,128)}, u32[]{:S(2)}) copy-start(s32[4,256]{1,0:T(4,128)} %param.20) | copy-start | bytes 12292
  7.9 28.9 %copy-start.133 = (s32[256]{0:T(256)S(1)}, s32[256]{0:T(256)}, u32[]{:S(2)}) copy-start(s32[256]{0:T(256)} %param.19) | copy-start | bytes 3076
  7.9 29.4 %copy-start.67 = (f32[3,9,9]{2,0,1:T(4,128)S(1)}, f32[3,9,9]{2,0,1:T(4,128)}, u32[]{:S(2)}) copy-start(f32[3,9,9]{2,0,1:T(4,128)} %param.26) | copy-start | bytes 2920
  7.9 29.4 %copy-start.127 = (s32[256]{0:T(256)S(1)}, s32[256]{0:T(256)}, u32[]{:S(2)}) copy-start(s32[256]{0:T(256)} %param.18) | copy-start | bytes 3076
  8.9 28.8 %copy-start.68 = (f32[3,9,9]{2,0,1:T(4,128)S(1)}, f32[3,9,9]{2,0,1:T(4,128)}, u32[]{:S(2)}) copy-start(f32[3,9,9]{2,0,1:T(4,128)} %param.27) | copy-start | bytes 2920
  8.9 29.2 %copy-start.135 = (s32[4,256]{1,0:T(4,128)S(1)}, s32[4,256]{1,0:T(4,128)}, u32[]{:S(2)}) copy-start(s32[4,256]{1,0:T(4,128)} %param.21) | copy-start | bytes 12292
  8.9 29.6 %copy-start.136 = (f32[4,256]{1,0:T(4,128)S(1)}, f32[4,256]{1,0:T(4,128)}, u32[]{:S(2)}) copy-start(f32[4,256]{1,0:T(4,128)} %param.17) | copy-start | bytes 12292
  8.9 30.2 %copy-start.66 = (f32[4,10,10]{2,0,1:T(4,128)S(1)}, f32[4,10,10]{2,0,1:T(4,128)}, u32[]{:S(2)}) copy-start(f32[4,10,10]{2,0,1:T(4,128)} %param.24) | copy-start | bytes 4804
  8.9 50.0 %collective-permute-start.1 = (f32[9,10,128]{2,1,0:T(8,128)S(1)}, f32[9,10,128]{2,1,0:T(8,128)S(1)}, u32[]{:S(2)}, u32[]{:S(2)}) collective-permute-start(f32[9,10,128]{2,1,0:T(8,128)S(1)} %get-tuple-element.348), channel_id=1, source_target_pairs={{8,0},{16,8},{24,16},{32,24},{40,32},{48,40},{56,48},{64,56},{72,6... | collective-permute-start | bytes 138248 | tf_op jit(solution)/shard_map/ppermute | solution.py:33
  25.8 33.2 %collective-permute-start = (f32[9,10,128]{2,1,0:T(8,128)S(1)}, f32[9,10,128]{2,1,0:T(8,128)S(1)}, u32[]{:S(2)}, u32[]{:S(2)}) collective-permute-start(f32[9,10,128]{2,1,0:T(8,128)S(1)} %get-tuple-element.347), channel_id=1, source_target_pairs={{760,0},{0,8},{8,16},{16,24},{24,32},{32,40},{40,48},{48,56},{56,6... | collective-permute-start | bytes 138248 | tf_op jit(solution)/shard_map/ppermute | solution.py:33
  28.7 28.4 %all-to-all-start = ((f32[8,1,5760]{2,1,0:T(1,128)}), f32[8,1,5760]{2,1,0:T(1,128)S(1)}, u32[]{:S(2)}, u32[]{:S(2)}) async-start(f32[8,1,5760]{2,1,0:T(1,128)} %reshape.169), calls=%async_computation | async-start | bytes 368640 | tf_op jit(solution)/shard_map/all_to_all | solution.py:21
  37.7 27.4 %copy-start.128 = (s32[1024]{0:T(1024)}, s32[1024]{0:T(1024)S(1)}, u32[]{:S(2)}) copy-start(s32[1024]{0:T(1024)S(1)} %pad_clamp_fusion) | copy-start | bytes 12292
  39.7 32.3 %copy-start.129 = (s32[1024]{0:T(1024)}, s32[1024]{0:T(1024)S(1)}, u32[]{:S(2)}) copy-start(s32[1024]{0:T(1024)S(1)} %pad_clamp_fusion.1) | copy-start | bytes 12292
  56.4 33.6 %copy-start.141 = (pred[256]{0:T(512)(128)(4,1)}, pred[256]{0:T(512)(128)(4,1)S(1)}, u32[]{:S(2)}) copy-start(pred[256]{0:T(512)(128)(4,1)S(1)} %compare_and_fusion.3) | copy-start | bytes 772
  56.4 29.4 %copy-start.130 = (s32[1024]{0:T(1024)}, s32[1024]{0:T(1024)S(1)}, u32[]{:S(2)}) copy-start(s32[1024]{0:T(1024)S(1)} %pad_clamp_fusion.3) | copy-start | bytes 12292
  103.8 23.0 %collective-permute-start.3 = (f32[9,10,128]{2,1,0:T(8,128)S(1)}, f32[9,10,128]{2,1,0:T(8,128)S(1)}, u32[]{:S(2)}, u32[]{:S(2)}) collective-permute-start(f32[9,10,128]{2,1,0:T(8,128)S(1)} %get-tuple-element.247), channel_id=1, source_target_pairs={{8,0},{16,8},{24,16},{32,24},{40,32},{48,40},{56,48},{64,56},{72,6... | collective-permute-start | bytes 138248 | tf_op jit(solution)/shard_map/ppermute | solution.py:33
  111.1 15.7 %collective-permute-start.2 = (f32[9,10,128]{2,1,0:T(8,128)S(1)}, f32[9,10,128]{2,1,0:T(8,128)S(1)}, u32[]{:S(2)}, u32[]{:S(2)}) collective-permute-start(f32[9,10,128]{2,1,0:T(8,128)S(1)} %get-tuple-element.246), channel_id=1, source_target_pairs={{760,0},{0,8},{8,16},{16,24},{24,32},{32,40},{40,48},{48,56},{56,6... | collective-permute-start | bytes 138248 | tf_op jit(solution)/shard_map/ppermute | solution.py:33
  114.0 11.4 %all-to-all-start.1 = ((f32[8,1,5760]{2,1,0:T(1,128)}), f32[8,1,5760]{2,1,0:T(1,128)S(1)}, u32[]{:S(2)}, u32[]{:S(2)}) async-start(f32[8,1,5760]{2,1,0:T(1,128)} %reshape.171), calls=%async_computation.1 | async-start | bytes 368640 | tf_op jit(solution)/shard_map/all_to_all | solution.py:21
  126.8 27.2 %copy-start.140 = (pred[256]{0:T(512)(128)(4,1)S(1)}, pred[256]{0:T(512)(128)(4,1)}, u32[]{:S(2)}) copy-start(pred[256]{0:T(512)(128)(4,1)} %compare_and_fusion) | copy-start | bytes 772
  (100 other events, 516.5 us)
where the time goes:
time: 187 us; the launch traced here: 185 us
  local copies, waits for them, and re-layouts  96.5 us (52%)
  starting transfers between devices  39.4 us (21%)
  matrix products  22.6 us (12%)
  other arithmetic  20.5 us (11%)
  between operations  3.42 us (2%)
  waiting for transfers between devices  2.58 us (1%)
    gather x8, local copies, waits for them, and re-layouts, advance(): parts = [jnp.take(table, neighbours[face], axis=2) for face in range(4)]  37.8 us
    ppermute x4, starting transfers between devices, from_behind(): return lax.ppermute(block, axis, route)  28 us
    unnamed x341, local copies, waits for them, and re-layouts  15.1 us
    dot_general x8, matrix products, update(): jnp.einsum('ab,vbe->vae', flux_local[face], plus, precision=lax.Precision...  12.5 us
    concatenate x2, local copies, waits for them, and re-layouts, integrate(): return (whole, jnp.concatenate([whole] + outside, axis=2))  12.2 us
    all_to_all x2, starting transfers between devices, sent_to_all(): lax.all_to_all(jnp.broadcast_to(value[None], (devices, *value.shape)), ax...  11.5 us
    mul x64, local copies, waits for them, and re-layouts, per_element(): total = total + matrix[:, inner][:, None, :] * values[inner][None, :, :]  10 us
    slice x12, local copies, waits for them, and re-layouts, per_element(): total = matrix[:, 0][:, None, :] * values[0][None, :, :]  8.11 us
  transfers between devices with their start and end apart: 6, of which 1 were waited for; matrix products, arithmetic and copies ran while one was open for 16% of the time, Pallas kernels for 0%

commit v1 on v0

v1 whole, which is shorter than its diff:
```python
import jax
import jax.numpy as jnp
from jax import lax
from jax.experimental import pallas as pl
from jax.experimental.pallas import tpu as pltpu
from jax.sharding import PartitionSpec as P

V = 9
B = 10
E = 256
COPY = 128
SUBC = 64
ROWS = 96
DT = 0.2
EXACT = lax.Precision.HIGHEST
f32 = jnp.float32
bf16 = jnp.bfloat16


def row_of(w, b):
    return w * 8 + b if b < 8 else 72 + 2 * w + b - 8


def by_material(material, pick):
    first = jnp.broadcast_to(material == 0, (V, E))
    second = jnp.broadcast_to(material == 1, (V, E))
    column = [jnp.broadcast_to(pick(m), (V, E)) for m in range(3)]
    return jnp.where(first, column[0], jnp.where(second, column[1], column[2]))


def mapped(matrix, values, out_ref):
    wide = jnp.concatenate(values, axis=1)
    out_ref[...] = jnp.dot(matrix, wide, precision=EXACT, preferred_element_type=f32)


def block(ref, row, w):
    return ref[16 * row : 16 * row + B, w * E : (w + 1) * E]


def mixed(total, matrix_ref, index, value):
    for v in range(V):
        term = matrix_ref[index, v : v + 1, :] * value
        total[v] = term if total[v] is None else total[v] + term


def star(values, matrix, jac_ref, y_ref):
    mapped(matrix, values, y_ref)
    total = [None] * V
    for i in range(3):
        for w in range(V):
            mixed(total, jac_ref, i * V + w, block(y_ref, i, w))
    return total


def padded_stiffness(stiffness_ref, k_ref):
    k_ref[...] = jnp.zeros_like(k_ref)
    for i in range(3):
        k_ref[16 * i : 16 * i + B, :] = stiffness_ref[i]


def pack(values, p_ref, lower_ref, upper_ref, sub_ref):
    for v in range(V):
        p_ref[8 * v : 8 * v + 8, :] = values[v][:8]
        p_ref[72 + 2 * v : 74 + 2 * v, :] = values[v][8:]
    p_ref[90:ROWS, :] = jnp.zeros((ROWS - 90, E), f32)
    low = p_ref[:, :COPY]
    lower_ref[...] = low
    upper_ref[...] = p_ref[:, COPY:]
    lane = lax.broadcasted_iota(jnp.int32, (48, 128), 1)
    sub_ref[...] = jnp.where(lane < SUBC, low[:48], pltpu.roll(low[48:], SUBC, 1))


def first_kernel(
    state_ref, geo_ref, mat_ref, jac_ref, stiff_ref,
    ejac_ref, j_ref, p_ref, lower_ref, upper_ref, sub_ref, k_ref, y_ref,
):
    material = mat_ref[...]
    padded_stiffness(stiff_ref, k_ref)
    for w in range(V):
        parts = [
            by_material(material, lambda m: jac_ref[m, c, :, w : w + 1]) for c in range(3)
        ]
        for i in range(3):
            ejac_ref[i * V + w] = (
                geo_ref[i, 0:1, :] * parts[0]
                + geo_ref[i, 1:2, :] * parts[1]
                + geo_ref[i, 2:3, :] * parts[2]
            )
    values = [state_ref[v] for v in range(V)]
    matrix = k_ref[...]
    one = star(values, matrix, ejac_ref, y_ref)
    two = star(one, matrix, ejac_ref, y_ref)
    out = []
    for v in range(V):
        integral = DT * state_ref[v] - DT**2 / 2 * one[v] + DT**3 / 6 * two[v]
        j_ref[v] = integral
        out.append(integral)
    pack(out, p_ref, lower_ref, upper_ref, sub_ref)


def split(values):
    high = values.astype(bf16)
    low = (values - high.astype(f32)).astype(bf16)
    return jnp.concatenate([high, low], axis=0)


def one_hot(index, start, count):
    places = lax.broadcasted_iota(jnp.int32, (count, E), 0) + start
    return jnp.where(places == index, 1.0, 0.0).astype(bf16)


def gathered(pieces, picks, n_ref):
    for face in range(4):
        both = jnp.dot(pieces, picks(face), preferred_element_type=f32)
        n_ref[:, face * E : (face + 1) * E] = both[:ROWS] + both[ROWS:]


def neighbour_flux(n_ref, turn_ref, minus_ref, total):
    for face in range(4):
        lanes = slice(face * E, (face + 1) * E)
        if face == 0:
            across = [None] * V
        for b in range(B):
            turn = turn_ref[face * B + b]
            for w in range(V):
                row = row_of(w, b)
                term = turn * n_ref[row : row + 1, lanes]
                across[w] = term if across[w] is None else across[w] + term
    for w in range(V):
        mixed(total, minus_ref, w, across[w])
    return total


def local_part(j_ref, p_ref, matrix, scale_ref, ejac_ref, plus_ref, minus_ref, turn_ref,
               picks, y_ref, n_ref, out_ref):
    mapped(matrix, [j_ref[v] for v in range(V)], y_ref)
    gathered(split(p_ref[...]), picks, n_ref)
    total = [None] * V
    for i in range(3):
        for w in range(V):
            mixed(total, ejac_ref, i * V + w, block(y_ref, i, w))
    for v in range(V):
        out_ref[v] = total[v]
    total = [None] * V
    for w in range(V):
        own = scale_ref[0:1, :] * block(y_ref, 3, w)
        for face in range(1, 4):
            own = own + scale_ref[face : face + 1, :] * block(y_ref, 3 + face, w)
        mixed(total, plus_ref, w, own)
    for v in range(V):
        out_ref[v] = out_ref[v] - total[v]
    total = neighbour_flux(n_ref, turn_ref, minus_ref, [None] * V)
    for v in range(V):
        out_ref[v] = out_ref[v] - total[v]


def local_kernel_one(
    j_ref, p_ref, ejac_ref, matrix_ref, mat_ref, near_ref, orient_ref, scale_ref,
    fplus_ref, fminus_ref, fneigh_ref,
    out_ref, plus_ref, minus_ref, turn_ref, here_ref, there_ref, y_ref, n_ref,
):
    material = mat_ref[...]
    for w in range(V):
        plus_ref[w] = by_material(material, lambda m: fplus_ref[m, :, w : w + 1])
        minus_ref[w] = by_material(material, lambda m: fminus_ref[m, :, w : w + 1])
    for face in range(4):
        index = near_ref[face : face + 1, :]
        here_ref[face] = one_hot(index, 0, E)
        there_ref[face] = one_hot(index, E, 768)
        way = orient_ref[face : face + 1, :]
        scale = scale_ref[face : face + 1, :]
        masks = [jnp.broadcast_to(way == t, (B, E)) for t in range(11)]
        for b in range(B):
            chosen = jnp.broadcast_to(fneigh_ref[11, :, b : b + 1], (B, E))
            for t in range(11):
                column = jnp.broadcast_to(fneigh_ref[t, :, b : b + 1], (B, E))
                chosen = jnp.where(masks[t], column, chosen)
            turn_ref[face * B + b] = chosen * scale
    local_part(j_ref, p_ref, matrix_ref[...], scale_ref, ejac_ref, plus_ref, minus_ref,
               turn_ref, lambda face: here_ref[face], y_ref, n_ref, out_ref)


def local_kernel_two(
    j_ref, p_ref, ejac_ref, matrix_ref, scale_ref, plus_ref, minus_ref, turn_ref, here_ref,
    out_ref, y_ref, n_ref,
):
    local_part(j_ref, p_ref, matrix_ref[...], scale_ref, ejac_ref, plus_ref, minus_ref,
               turn_ref, lambda face: here_ref[face], y_ref, n_ref, out_ref)


def remote_flux(group_ref, left_ref, right_ref, there_ref, turn_ref, minus_ref, n_ref):
    lane = lax.broadcasted_iota(jnp.int32, (48, 128), 1)
    table = []
    for pair in range(4):
        one = group_ref[2 * pair]
        two = group_ref[2 * pair + 1]
        top = jnp.where(lane < SUBC, one, pltpu.roll(two, SUBC, 1))
        bottom = jnp.where(lane < SUBC, pltpu.roll(one, SUBC, 1), two)
        table.append(jnp.concatenate([top, bottom], axis=0))
    table += [left_ref[...], right_ref[...]]
    pieces = split(jnp.concatenate(table, axis=1))
    gathered(pieces, lambda face: there_ref[face], n_ref)
    return neighbour_flux(n_ref, turn_ref, minus_ref, [None] * V)


def middle_kernel(
    state_ref, local_ref, group_ref, left_ref, right_ref, there_ref, turn_ref, minus_ref,
    ejac_ref, stiff_ref, cluster_ref,
    base_ref, j_ref, p_ref, lower_ref, upper_ref, sub_ref, n_ref, k_ref, y_ref, m_ref,
):
    flux = remote_flux(group_ref, left_ref, right_ref, there_ref, turn_ref, minus_ref, n_ref)
    coarse = cluster_ref[...].astype(f32)
    fine = 1.0 - coarse
    for v in range(V):
        change = local_ref[v] - flux[v]
        base_ref[v] = state_ref[v] + change
        m_ref[v] = state_ref[v] + fine * change
    padded_stiffness(stiff_ref, k_ref)
    matrix = k_ref[...]
    one = star([m_ref[v] for v in range(V)], matrix, ejac_ref, y_ref)
    two = star(one, matrix, ejac_ref, y_ref)
    weight_one = DT**2 / 2 + DT**2 * coarse
    weight_two = DT**3 / 6 + DT**3 * coarse
    out = []
    for v in range(V):
        integral = DT * m_ref[v] - weight_one * one[v] + weight_two * two[v]
        j_ref[v] = integral
        out.append(integral)
    pack(out, p_ref, lower_ref, upper_ref, sub_ref)


def last_kernel(
    base_ref, local_ref, group_ref, left_ref, right_ref, there_ref, turn_ref, minus_ref,
    out_ref, n_ref,
):
    flux = remote_flux(group_ref, left_ref, right_ref, there_ref, turn_ref, minus_ref, n_ref)
    for v in range(V):
        out_ref[v] = base_ref[v] + (local_ref[v] - flux[v])


def arr(*shape, dtype=f32):
    return jax.ShapeDtypeStruct(shape, dtype)


def call(kernel, outs, scratch, flops, name):
    return pl.pallas_call(
        kernel,
        out_shape=outs,
        scratch_shapes=[pltpu.VMEM(s, f32) for s in scratch],
        compiler_params=pltpu.CompilerParams(vmem_limit_bytes=24 << 20),
        cost_estimate=pl.CostEstimate(flops=flops, bytes_accessed=1 << 20, transcendentals=0),
        name=name,
    )


def sent(value, axis, shift):
    size = lax.axis_size(axis)
    return lax.ppermute(value, axis, [((i - shift) % size, i) for i in range(size)])


def exchange(lower, upper, sub):
    left = sent(upper, "dom", 1)
    right = sent(lower, "dom", -1)
    group = lax.all_to_all(
        jnp.broadcast_to(sub[None], (8, *sub.shape)), "sub", 0, 0, tiled=True
    )
    return group, left, right


def shards(state, geometry, face_scale, material, cluster, neighbours, orientation,
           stiffness, jacobians, flux_local, flux_neigh, flux_plus, flux_minus):
    material = material.reshape(1, E)
    cluster = cluster.reshape(1, E)
    cube = arr(V, B, E)
    packed = [arr(ROWS, E), arr(ROWS, COPY), arr(ROWS, COPY), arr(48, 128)]
    wide = (112, V * E)
    narrow = (48, V * E)
    picked = (ROWS, 4 * E)

    ejac, j0, p0, lower, upper, sub = call(
        first_kernel, [arr(27, V, E), cube, *packed], [(48, B), narrow], 1 << 28, "first"
    )(state, geometry, material, jacobians, stiffness)
    remote0 = exchange(lower, upper, sub)
    matrix = jnp.concatenate([jnp.swapaxes(stiffness, 1, 2), flux_local], axis=0)
    matrix = jnp.pad(matrix, ((0, 0), (0, 6), (0, 0))).reshape(112, B)
    local0, plus, minus, turn, here, there = call(
        local_kernel_one,
        [cube, arr(V, V, E), arr(V, V, E), arr(4 * B, B, E),
         arr(4, E, E, dtype=bf16), arr(4, 768, E, dtype=bf16)],
        [wide, picked], 1 << 33, "local_one",
    )(j0, p0, ejac, matrix, material, neighbours, orientation, face_scale,
      flux_plus, flux_minus, flux_neigh)
    base, j1, p1, lower, upper, sub = call(
        middle_kernel, [cube, cube, *packed],
        [picked, (48, B), narrow, (V, B, E)], 1 << 28, "middle",
    )(state, local0, *remote0, there, turn, minus, ejac, stiffness, cluster)
    remote1 = exchange(lower, upper, sub)
    local1 = call(local_kernel_two, cube, [wide, picked], 1 << 33, "local_two")(
        j1, p1, ejac, matrix, face_scale, plus, minus, turn, here
    )
    return call(last_kernel, cube, [picked], 1 << 28, "last")(
        base, local1, *remote1, there, turn, minus
    )


def solution(mesh):
    whole = ("dom", "sub")
    placed = (
        P(None, None, whole), P(None, None, whole), P(None, whole), P(whole), P(whole),
        P(None, whole), P(None, whole), P(), P(), P(), P(), P(), P(),
    )
    return jax.shard_map(
        shards, mesh=mesh, in_specs=placed, out_specs=P(None, None, whole), check_vma=False
    )
```

time: 187 us -> 68.9 us (0.37)
  local copies, waits for them, and re-layouts: 96.5 us -> 15.9 us
  matrix products: 22.6 us -> 0 us
  other arithmetic: 20.5 us -> 0.02 us
  Pallas kernels: 0 us -> 11.6 us
  between operations: 3.42 us -> 0.28 us
  waiting for transfers between devices: 2.58 us -> 0.28 us
    gather x8 -> x0, local copies, waits for them, and re-layouts: 37.8 us -> none  [advance(): parts = [jnp.take(table, neighbours[face], axis=2) for face in range(4)]]
    dot_general x33 -> x0, matrix products: 22.6 us -> none  [the longest x8 12.5 us: update(): jnp.einsum('ab,vbe->vae', flux_local[face], plus, precision=lax.Precision...]
    mul x99 -> x0, local copies, waits for them, and re-layouts: 19 us -> none  [the longest x64 10 us: per_element(): total = total + matrix[:, inner][:, None, :] * values[inner][None, :, :]]
    concatenate x2 -> x0, local copies, waits for them, and re-layouts: 12.2 us -> none  [integrate(): return (whole, jnp.concatenate([whole] + outside, axis=2))]
    pallas_call x0 -> x5, Pallas kernels: none -> 11.6 us  [the longest x1 3.68 us: shards(): call(middle_kernel, [cube, cube, *packed], [picked, (48, B), narrow, (V,...]
    slice x26 -> x0, local copies, waits for them, and re-layouts: 11.4 us -> none  [the longest x12 8.11 us: per_element(): total = matrix[:, 0][:, None, :] * values[0][None, :, :]]
    select_n x12 -> x0, other arithmetic: 8.1 us -> none  [advance(): parts = [jnp.take(table, neighbours[face], axis=2) for face in range(4)]]
    add x12 -> x0, other arithmetic: 6.17 us -> none  [the longest x10 3.94 us: per_element(): total = total + matrix[:, inner][:, None, :] * values[inner][None, :, :]]
  transfers between devices with their start and end apart: 6 -> 6, of which waited for: 1 -> 1; matrix products, arithmetic and copies ran while one was open for 16% -> 2% of each run, Pallas kernels for 0% -> 6%
where the time goes in v1:
time: 68.9 us; the launch traced here: 68.1 us
  starting transfers between devices  40 us (58%)
  local copies, waits for them, and re-layouts  15.9 us (23%)
  Pallas kernels  11.6 us (17%)
    ppermute x4, starting transfers between devices, sent(): lax.ppermute(value, axis, [((i - shift) % size, i) for i in range(size)])  28.5 us
    unnamed x63, local copies, waits for them, and re-layouts  14.5 us
    all_to_all x2, starting transfers between devices, exchange(): lax.all_to_all(jnp.broadcast_to(sub[None], (8, *sub.shape)), 'sub', 0, 0,...  11.5 us
    pallas_call x1, Pallas kernels, shards(): call(middle_kernel, [cube, cube, *packed], [picked, (48, B), narrow, (V,...  3.68 us
    pallas_call x1, Pallas kernels, shards(): call(local_kernel_one, [cube, arr(V, V, E), arr(V, V, E), arr(4 * B, B, E...  2.64 us
    pallas_call x1, Pallas kernels, shards(): call(first_kernel, [arr(27, V, E), cube, *packed], [(48, B), narrow], 1 <...  1.99 us
    pallas_call x1, Pallas kernels, shards(): call(local_kernel_two, cube, [wide, picked], 1 << 33, 'local_two')  1.72 us
    pallas_call x1, Pallas kernels, shards(): call(last_kernel, cube, [picked], 1 << 28, 'last')  1.6 us
  transfers between devices with their start and end apart: 6, of which 1 were waited for; matrix products, arithmetic and copies ran while one was open for 2% of the time, Pallas kernels for 6%

profile of v1, /device:TPU:8, one launch (start us, length us, event | category | flops | bytes accessed | tf_op | source)
XLA Modules:
  0.0 68.1 jit_solution(7757857096132972693)
XLA Ops:
  0.0 0.0 copy-start.27
  0.0 0.0 copy-start.23
  0.0 0.0 copy-start.12
  0.0 0.0 copy-start.11
  0.0 0.0 copy-start.10
  0.1 0.8 %copy.15.stiff_ref = f32[3,10,10]{2,1,0:T(8,128)S(1)} copy(f32[3,10,10]{2,0,1:T(4,128)} %param.20) | data formatting | bytes 2400 | tf_op args[7]
  0.9 0.8 %copy.14.jac_ref = f32[3,3,9,9]{3,2,1,0:T(8,128)S(1)} copy(f32[3,3,9,9]{3,1,2,0:T(4,128)} %param.21) | data formatting | bytes 5832 | tf_op args[8]
  1.7 0.9 %copy-done = f32[9,10,256]{2,1,0:T(8,128)S(1)} copy-done((f32[9,10,256]{2,1,0:T(8,128)S(1)}, f32[9,10,256]{2,1,0:T(8,128)}, u32[]{:S(2)}) %copy-start) | copy-done | bytes 92184
  2.6 0.7 %copy-done.9 = f32[3,3,256]{2,1,0:T(4,128)S(1)} copy-done((f32[3,3,256]{2,1,0:T(4,128)S(1)}, f32[3,3,256]{2,1,0:T(4,128)}, u32[]{:S(2)}) %copy-start.9) | copy-done | bytes 9240
  3.3 0.7 copy-done.13
  4.0 2.0 %first.1 = (f32[27,9,256]{2,1,0:T(8,128)S(1)}, f32[9,10,256]{2,1,0:T(8,128)S(1)}, f32[96,256]{1,0:T(8,128)S(1)}, f32[96,128]{1,0:T(8,128)}, f32[96,128]{1,0:T(8,128)}, /*index=5*/f32[48,128]{1,0:T(8,128)S(1)}) custom-call(f32[9,10,256]{2,1,0:T(8,128)S(1)} %copy-done, f32[3,3,256]{2,1,0:T(4,128)S(1)} %copy-done.9, s32[1,256]{1,0:T(1,128)S(1)} %bitcast.7, ...), custom_call_target="tpu_custom_call" | custom-call | flops 268435456 | bytes 1048576 | tf_op jit(solution)/shard_map/first/pallas_call | solution.py:280
  6.0 1.9 %collective-permute-start = (f32[96,128]{1,0:T(8,128)}, f32[96,128]{1,0:T(8,128)S(1)}, u32[]{:S(2)}, u32[]{:S(2)}) collective-permute-start(f32[96,128]{1,0:T(8,128)} %get-tuple-element.28), channel_id=1, source_target_pairs={{760,0},{0,8},{8,16},{16,24},{24,32},{32,40},{40,48},{48,56},{56,6... | collective-permute-start | bytes 147464 | tf_op jit(solution)/shard_map/ppermute | solution.py:258
  7.9 16.8 %collective-permute-start.1 = (f32[96,128]{1,0:T(8,128)}, f32[96,128]{1,0:T(8,128)}, u32[]{:S(2)}, u32[]{:S(2)}) collective-permute-start(f32[96,128]{1,0:T(8,128)} %get-tuple-element.29), channel_id=1, source_target_pairs={{8,0},{16,8},{24,16},{32,24},{40,32},{48,40},{56,48},{64,56},{72,6... | collective-permute-start | bytes 147464 | tf_op jit(solution)/shard_map/ppermute | solution.py:258
  24.7 0.7 %broadcast_in_dim.4 = f32[8,48,128]{2,1,0:T(8,128)} broadcast(f32[48,128]{1,0:T(8,128)S(1)} %get-tuple-element.27), dimensions={1,2} | broadcast | bytes 221184 | tf_op jit(solution)/shard_map/broadcast_in_dim | solution.py:265
  25.4 5.8 %all-to-all-start = ((f32[8,48,128]{2,1,0:T(8,128)}), f32[8,48,128]{2,1,0:T(8,128)S(1)}, u32[]{:S(2)}, u32[]{:S(2)}) async-start(f32[8,48,128]{2,1,0:T(8,128)} %broadcast_in_dim.4), calls=%async_computation | async-start | bytes 393216 | tf_op jit(solution)/shard_map/all_to_all | solution.py:264
  31.2 0.0 copy-done.24
  31.2 0.1 copy.16
  31.5 0.0 copy-start.14
  31.5 0.7 copy-done.14
  32.2 0.9 %copy-done.16 = f32[9,10,256]{2,1,0:T(8,128)S(1)} copy-done((f32[9,10,256]{2,1,0:T(8,128)S(1)}, f32[9,10,256]{2,1,0:T(8,128)}, u32[]{:S(2)}) %copy-start.16) | copy-done | bytes 92184
  33.1 0.9 %copy-done.18 = f32[96,256]{1,0:T(8,128)S(1)} copy-done((f32[96,256]{1,0:T(8,128)S(1)}, f32[96,256]{1,0:T(8,128)}, u32[]{:S(2)}) %copy-start.18) | copy-done | bytes 98328
  34.0 2.6 %local_one.1 = (f32[9,10,256]{2,1,0:T(8,128)S(1)}, f32[9,9,256]{2,1,0:T(8,128)S(1)}, f32[9,9,256]{2,1,0:T(8,128)S(1)}, f32[40,10,256]{2,1,0:T(8,128)S(1)}, bf16[...) custom-call(f32[9,10,256]{2,1,0:T(8,128)S(1)} %copy-done.16, f32[96,256]{1,0:T(8,128)S(1)} %copy-done.18, ...), custom_call_target="tpu_custom_call" | custom-call | flops 8589934592 | bytes 1048576 | tf_op jit(solution)/shard_map/local_one/pallas_call | solution.py:286
  36.6 0.8 %copy-done.19 = bf16[4,256,256]{2,1,0:T(8,128)(2,1)} copy-done((bf16[4,256,256]{2,1,0:T(8,128)(2,1)}, bf16[4,256,256]{2,1,0:T(8,128)(2,1)S(1)}, u32[]{:S(2)}) %copy-start.19) | copy-done | bytes 524312
  37.4 0.7 copy-done.21
  38.1 0.0 collective-permute-done.left_ref
  38.1 0.6 copy-done.2
  38.7 0.0 collective-permute-done.1.right_ref
  38.7 0.0 all-to-all-done.group_ref
  38.7 0.0 copy-done.1
  38.7 0.0 copy-done.4
  38.7 0.0 copy-start.3
  38.7 0.8 %copy-done.3 = f32[96,128]{1,0:T(8,128)S(1)} copy-done((f32[96,128]{1,0:T(8,128)S(1)}, f32[96,128]{1,0:T(8,128)}, u32[]{:S(2)}) %copy-start.3) | copy-done | bytes 49176
  39.5 3.7 %middle.1 = (f32[9,10,256]{2,1,0:T(8,128)S(1)}, f32[9,10,256]{2,1,0:T(8,128)S(1)}, f32[96,256]{1,0:T(8,128)S(1)}, f32[96,128]{1,0:T(8,128)}, f32[96,128]{1,0:T(8,128)}, /*index=5*/f32[48,128]{1,0:T(8,128)S(1)}) custom-call(f32[9,10,256]{2,1,0:T(8,128)S(1)} %copy-done.1, f32[9,10,256]{2,1,0:T(8,128)S(1)} %get-tuple-element.26.local_ref, ...), custom_call_target="tpu_custom_call" | custom-call | flops 268435456 | bytes 1048576 | tf_op jit(solution)/shard_map/middle/pallas_call | solution.py:293
  43.2 0.7 copy-done.5
  43.9 0.6 copy-done.7
  44.5 1.9 %collective-permute-start.2 = (f32[96,128]{1,0:T(8,128)}, f32[96,128]{1,0:T(8,128)S(1)}, u32[]{:S(2)}, u32[]{:S(2)}) collective-permute-start(f32[96,128]{1,0:T(8,128)} %get-tuple-element.39), channel_id=1, source_target_pairs={{760,0},{0,8},{8,16},{16,24},{24,32},{32,40},{40,48},{48,56},{56,6... | collective-permute-start | bytes 147464 | tf_op jit(solution)/shard_map/ppermute | solution.py:258
  46.4 7.9 %collective-permute-start.3 = (f32[96,128]{1,0:T(8,128)}, f32[96,128]{1,0:T(8,128)S(1)}, u32[]{:S(2)}, u32[]{:S(2)}) collective-permute-start(f32[96,128]{1,0:T(8,128)} %get-tuple-element.40), channel_id=1, source_target_pairs={{8,0},{16,8},{24,16},{32,24},{40,32},{48,40},{56,48},{64,56},{72,6... | collective-permute-start | bytes 147464 | tf_op jit(solution)/shard_map/ppermute | solution.py:258
  54.3 0.7 %broadcast_in_dim.5 = f32[8,48,128]{2,1,0:T(8,128)} broadcast(f32[48,128]{1,0:T(8,128)S(1)} %get-tuple-element.38), dimensions={1,2} | broadcast | bytes 221184 | tf_op jit(solution)/shard_map/broadcast_in_dim | solution.py:265
  55.0 5.7 %all-to-all-start.1 = ((f32[8,48,128]{2,1,0:T(8,128)}), f32[8,48,128]{2,1,0:T(8,128)S(1)}, u32[]{:S(2)}, u32[]{:S(2)}) async-start(f32[8,48,128]{2,1,0:T(8,128)} %broadcast_in_dim.5), calls=%async_computation.1 | async-start | bytes 393216 | tf_op jit(solution)/shard_map/all_to_all | solution.py:264
  60.7 0.9 %copy-done.6 = f32[9,10,256]{2,1,0:T(8,128)S(1)} copy-done((f32[9,10,256]{2,1,0:T(8,128)S(1)}, f32[9,10,256]{2,1,0:T(8,128)}, u32[]{:S(2)}) %copy-start.6) | copy-done | bytes 92184
  61.6 0.9 %copy-done.8 = f32[96,256]{1,0:T(8,128)S(1)} copy-done((f32[96,256]{1,0:T(8,128)S(1)}, f32[96,256]{1,0:T(8,128)}, u32[]{:S(2)}) %copy-start.8) | copy-done | bytes 98328
  62.5 1.0 %copy-done.20 = bf16[4,256,256]{2,1,0:T(8,128)(2,1)S(1)} copy-done((bf16[4,256,256]{2,1,0:T(8,128)(2,1)S(1)}, bf16[4,256,256]{2,1,0:T(8,128)(2,1)}, u32[]{:S(2)}) %copy-start.20) | copy-done | bytes 524312
  63.5 0.9 %copy-done.22 = f32[9,9,256]{2,1,0:T(8,128)S(1)} copy-done((f32[9,9,256]{2,1,0:T(8,128)S(1)}, f32[9,9,256]{2,1,0:T(8,128)}, u32[]{:S(2)}) %copy-start.22) | copy-done | bytes 82968
  64.4 1.7 %local_two.1.local_ref = f32[9,10,256]{2,1,0:T(8,128)S(1)} custom-call(f32[9,10,256]{2,1,0:T(8,128)S(1)} %copy-done.6, f32[96,256]{1,0:T(8,128)S(1)} %copy-done.8, f32[27,9,256]{2,1,0:T(8,128)S(1)} %get-tuple-element.25.ejac_ref, f32[112,10]{1,0:T(8,128)S(1)} %bitcast.5, f32[4,256]{1,0:T(4,128)S(1)} %copy-done.12, f32[9,9,256]{2,1,0:T(8,128)S(1)} %copy-done.22, ...), custom_call_target="tpu_custom_call" | custom-call | flops 8589934592 | bytes 1048576 | tf_op jit(solution)/shard_map/local_two/pallas_call | solution.py:298
  66.2 0.0 collective-permute-done.2.left_ref
  66.2 0.0 collective-permute-done.3.right_ref
  66.2 0.3 all-to-all-done.1.group_ref
  66.5 1.6 %last.1 = f32[9,10,256]{2,1,0:T(8,128)} custom-call(f32[9,10,256]{2,1,0:T(8,128)S(1)} %get-tuple-element.33.base_ref, f32[9,10,256]{2,1,0:T(8,128)S(1)} %local_two.1.local_ref, f32[8,48,128]{2,1,0:T(8,128)S(1)} %all-to-all-done.1.group_ref, f32[96,128]{1,0:T(8,128)S(1)} %collective-permute-done.2.left_ref, f32[96,128]{1,0:T(8,128)S(1)} %collective-permute-done.3.right_ref, ...), custom_call_target="tpu_custom_call" | custom-call | flops 268435456 | bytes 1048576 | tf_op jit(solution)/shard_map/last/pallas_call | solution.py:301
  (36 shorter events, 0.1 us)
Async XLA Ops:
  0.0 31.2 %copy-start.24 = (f32[3,10,10]{2,0,1:T(4,128)S(1)}, f32[3,10,10]{2,0,1:T(4,128)}, u32[]{:S(2)}) copy-start(f32[3,10,10]{2,0,1:T(4,128)} %param.20) | copy-start | bytes 3604
  0.0 31.3 %copy-start.25 = (f32[4,10,10]{2,0,1:T(4,128)S(1)}, f32[4,10,10]{2,0,1:T(4,128)}, u32[]{:S(2)}) copy-start(f32[4,10,10]{2,0,1:T(4,128)} %param.22) | copy-start | bytes 4804
  0.0 31.3 %copy-start.26 = (f32[3,9,9]{2,0,1:T(4,128)S(1)}, f32[3,9,9]{2,0,1:T(4,128)}, u32[]{:S(2)}) copy-start(f32[3,9,9]{2,0,1:T(4,128)} %param.24) | copy-start | bytes 2920
  0.0 31.4 %copy-start.27 = (f32[3,9,9]{2,0,1:T(4,128)S(1)}, f32[3,9,9]{2,0,1:T(4,128)}, u32[]{:S(2)}) copy-start(f32[3,9,9]{2,0,1:T(4,128)} %param.25) | copy-start | bytes 2920
  0.0 31.4 %copy-start.23 = (f32[12,10,10]{2,0,1:T(8,128)S(1)}, f32[12,10,10]{2,0,1:T(8,128)}, u32[]{:S(2)}) copy-start(f32[12,10,10]{2,0,1:T(8,128)} %param.23) | copy-start | bytes 14404
  0.0 31.4 %copy-start.12 = (f32[4,256]{1,0:T(4,128)S(1)}, f32[4,256]{1,0:T(4,128)}, u32[]{:S(2)}) copy-start(f32[4,256]{1,0:T(4,128)} %scale_ref.3) | copy-start | bytes 12292
  0.0 31.4 %copy-start.11 = (s32[4,256]{1,0:T(4,128)S(1)}, s32[4,256]{1,0:T(4,128)}, u32[]{:S(2)}) copy-start(s32[4,256]{1,0:T(4,128)} %orient_ref.1) | copy-start | bytes 12292
  0.0 31.4 %copy-start.10 = (s32[4,256]{1,0:T(4,128)S(1)}, s32[4,256]{1,0:T(4,128)}, u32[]{:S(2)}) copy-start(s32[4,256]{1,0:T(4,128)} %near_ref.1) | copy-start | bytes 12292
  1.7 0.9 %copy-start = (f32[9,10,256]{2,1,0:T(8,128)S(1)}, f32[9,10,256]{2,1,0:T(8,128)}, u32[]{:S(2)}) copy-start(f32[9,10,256]{2,1,0:T(8,128)} %state_ref.3) | copy-start | bytes 276484
  2.6 0.7 %copy-start.9 = (f32[3,3,256]{2,1,0:T(4,128)S(1)}, f32[3,3,256]{2,1,0:T(4,128)}, u32[]{:S(2)}) copy-start(f32[3,3,256]{2,1,0:T(4,128)} %geo_ref.1) | copy-start | bytes 27652
  3.3 0.7 copy-start.13
  6.0 25.4 %copy-start.15 = (f32[9,10,256]{2,1,0:T(8,128)}, f32[9,10,256]{2,1,0:T(8,128)S(1)}, u32[]{:S(2)}) copy-start(f32[9,10,256]{2,1,0:T(8,128)S(1)} %get-tuple-element.23.j_ref) | copy-start | bytes 276484
  6.0 25.5 %copy-start.17 = (f32[96,256]{1,0:T(8,128)}, f32[96,256]{1,0:T(8,128)S(1)}, u32[]{:S(2)}) copy-start(f32[96,256]{1,0:T(8,128)S(1)} %get-tuple-element.24.p_ref) | copy-start | bytes 294916
  6.0 32.1 %collective-permute-start = (f32[96,128]{1,0:T(8,128)}, f32[96,128]{1,0:T(8,128)S(1)}, u32[]{:S(2)}, u32[]{:S(2)}) collective-permute-start(f32[96,128]{1,0:T(8,128)} %get-tuple-element.28), channel_id=1, source_target_pairs={{760,0},{0,8},{8,16},{16,24},{24,32},{32,40},{40,48},{48,56},{56,6... | collective-permute-start | bytes 147464 | tf_op jit(solution)/shard_map/ppermute | solution.py:258
  7.9 30.8 %collective-permute-start.1 = (f32[96,128]{1,0:T(8,128)}, f32[96,128]{1,0:T(8,128)}, u32[]{:S(2)}, u32[]{:S(2)}) collective-permute-start(f32[96,128]{1,0:T(8,128)} %get-tuple-element.29), channel_id=1, source_target_pairs={{8,0},{16,8},{24,16},{32,24},{40,32},{48,40},{56,48},{64,56},{72,6... | collective-permute-start | bytes 147464 | tf_op jit(solution)/shard_map/ppermute | solution.py:258
  25.4 13.3 %all-to-all-start = ((f32[8,48,128]{2,1,0:T(8,128)}), f32[8,48,128]{2,1,0:T(8,128)S(1)}, u32[]{:S(2)}, u32[]{:S(2)}) async-start(f32[8,48,128]{2,1,0:T(8,128)} %broadcast_in_dim.4), calls=%async_computation | async-start | bytes 393216 | tf_op jit(solution)/shard_map/all_to_all | solution.py:264
  31.5 0.7 %copy-start.14 = (s32[256]{0:T(256)S(1)}, s32[256]{0:T(256)}, u32[]{:S(2)}) copy-start(s32[256]{0:T(256)} %param.16) | copy-start | bytes 3076
  32.2 0.9 %copy-start.16 = (f32[9,10,256]{2,1,0:T(8,128)S(1)}, f32[9,10,256]{2,1,0:T(8,128)}, u32[]{:S(2)}) copy-start(f32[9,10,256]{2,1,0:T(8,128)} %copy-done.15) | copy-start | bytes 276484
  33.1 0.9 %copy-start.18 = (f32[96,256]{1,0:T(8,128)S(1)}, f32[96,256]{1,0:T(8,128)}, u32[]{:S(2)}) copy-start(f32[96,256]{1,0:T(8,128)} %copy-done.17) | copy-start | bytes 294916
  34.0 4.8 %copy-start.1 = (f32[9,10,256]{2,1,0:T(8,128)S(1)}, f32[9,10,256]{2,1,0:T(8,128)}, u32[]{:S(2)}) copy-start(f32[9,10,256]{2,1,0:T(8,128)} %state_ref.3) | copy-start | bytes 276484
  34.0 4.8 %copy-start.4 = (s32[256]{0:T(256)S(1)}, s32[256]{0:T(256)}, u32[]{:S(2)}) copy-start(s32[256]{0:T(256)} %param.17) | copy-start | bytes 3076
  36.6 0.8 %copy-start.19 = (bf16[4,256,256]{2,1,0:T(8,128)(2,1)}, bf16[4,256,256]{2,1,0:T(8,128)(2,1)S(1)}, u32[]{:S(2)}) copy-start(bf16[4,256,256]{2,1,0:T(8,128)(2,1)S(1)} %get-tuple-element.37.here_ref) | copy-start | bytes 1572868
  37.4 0.7 copy-start.21
  38.1 0.6 copy-start.2
  38.7 0.8 %copy-start.3 = (f32[96,128]{1,0:T(8,128)S(1)}, f32[96,128]{1,0:T(8,128)}, u32[]{:S(2)}) copy-start(f32[96,128]{1,0:T(8,128)} %copy-done.2) | copy-start | bytes 147460
  43.2 0.7 copy-start.5
  43.9 0.6 copy-start.7
  44.5 21.7 %collective-permute-start.2 = (f32[96,128]{1,0:T(8,128)}, f32[96,128]{1,0:T(8,128)S(1)}, u32[]{:S(2)}, u32[]{:S(2)}) collective-permute-start(f32[96,128]{1,0:T(8,128)} %get-tuple-element.39), channel_id=1, source_target_pairs={{760,0},{0,8},{8,16},{16,24},{24,32},{32,40},{40,48},{48,56},{56,6... | collective-permute-start | bytes 147464 | tf_op jit(solution)/shard_map/ppermute | solution.py:258
  46.4 19.8 %collective-permute-start.3 = (f32[96,128]{1,0:T(8,128)}, f32[96,128]{1,0:T(8,128)S(1)}, u32[]{:S(2)}, u32[]{:S(2)}) collective-permute-start(f32[96,128]{1,0:T(8,128)} %get-tuple-element.40), channel_id=1, source_target_pairs={{8,0},{16,8},{24,16},{32,24},{40,32},{48,40},{56,48},{64,56},{72,6... | collective-permute-start | bytes 147464 | tf_op jit(solution)/shard_map/ppermute | solution.py:258
  55.0 11.5 %all-to-all-start.1 = ((f32[8,48,128]{2,1,0:T(8,128)}), f32[8,48,128]{2,1,0:T(8,128)S(1)}, u32[]{:S(2)}, u32[]{:S(2)}) async-start(f32[8,48,128]{2,1,0:T(8,128)} %broadcast_in_dim.5), calls=%async_computation.1 | async-start | bytes 393216 | tf_op jit(solution)/shard_map/all_to_all | solution.py:264
  60.7 0.9 %copy-start.6 = (f32[9,10,256]{2,1,0:T(8,128)S(1)}, f32[9,10,256]{2,1,0:T(8,128)}, u32[]{:S(2)}) copy-start(f32[9,10,256]{2,1,0:T(8,128)} %copy-done.5) | copy-start | bytes 276484
  61.6 0.9 %copy-start.8 = (f32[96,256]{1,0:T(8,128)S(1)}, f32[96,256]{1,0:T(8,128)}, u32[]{:S(2)}) copy-start(f32[96,256]{1,0:T(8,128)} %copy-done.7) | copy-start | bytes 294916
  62.5 1.0 %copy-start.20 = (bf16[4,256,256]{2,1,0:T(8,128)(2,1)S(1)}, bf16[4,256,256]{2,1,0:T(8,128)(2,1)}, u32[]{:S(2)}) copy-start(bf16[4,256,256]{2,1,0:T(8,128)(2,1)} %copy-done.19) | copy-start | bytes 1572868
  63.5 0.9 %copy-start.22 = (f32[9,9,256]{2,1,0:T(8,128)S(1)}, f32[9,9,256]{2,1,0:T(8,128)}, u32[]{:S(2)}) copy-start(f32[9,9,256]{2,1,0:T(8,128)} %copy-done.21) | copy-start | bytes 248836

commit v2 on v1

v2 whole, which is shorter than its diff:
```python
import jax
import jax.numpy as jnp
from jax import lax
from jax.experimental import pallas as pl
from jax.experimental.pallas import tpu as pltpu
from jax.sharding import PartitionSpec as P

V = 9
B = 10
E = 256
COPY = 128
SUBC = 64
ROWS = 96
DT = 0.2
EXACT = lax.Precision.HIGH
f32 = jnp.float32
bf16 = jnp.bfloat16


def row_of(w, b):
    return w * 8 + b if b < 8 else 72 + 2 * w + b - 8


def by_material(material, pick):
    first = jnp.broadcast_to(material == 0, (V, E))
    second = jnp.broadcast_to(material == 1, (V, E))
    column = [jnp.broadcast_to(pick(m), (V, E)) for m in range(3)]
    return jnp.where(first, column[0], jnp.where(second, column[1], column[2]))


def mapped(matrix, values, out_ref):
    wide = jnp.concatenate(values, axis=1)
    out_ref[...] = jnp.dot(matrix, wide, precision=EXACT, preferred_element_type=f32)


def block(ref, row, w):
    return ref[16 * row : 16 * row + B, w * E : (w + 1) * E]


def mixed(total, matrix_ref, index, value):
    for v in range(V):
        row = index * V + v
        term = matrix_ref[row : row + 1, :] * value
        total[v] = term if total[v] is None else total[v] + term


def star(values, matrix, jac_ref, y_ref):
    mapped(matrix, values, y_ref)
    total = [None] * V
    for i in range(3):
        for w in range(V):
            mixed(total, jac_ref, i * V + w, block(y_ref, i, w))
    return total


def padded_stiffness(stiffness_ref, k_ref):
    k_ref[...] = jnp.zeros_like(k_ref)
    for a in range(B):
        for i in range(3):
            k_ref[16 * i + a : 16 * i + a + 1, :] = stiffness_ref[a, i : i + 1, :]


def by_matrix(rows_ref, out_ref):
    for a in range(rows_ref.shape[0]):
        for t in range(rows_ref.shape[1]):
            out_ref[t, a : a + 1, :] = rows_ref[a, t : t + 1, :]


def is_even():
    return lax.rem(lax.axis_index("dom"), 2) == 0


def pack(values, p_ref, outer_ref, inner_ref, sub_ref):
    for v in range(V):
        p_ref[8 * v : 8 * v + 8, :] = values[v][:8]
        p_ref[72 + 2 * v : 74 + 2 * v, :] = values[v][8:]
    p_ref[90:ROWS, :] = jnp.zeros((ROWS - 90, E), f32)
    low = p_ref[:, :COPY]
    high = p_ref[:, COPY:]
    even = is_even()
    outer_ref[...] = jnp.where(even, low, high)
    inner_ref[...] = jnp.where(even, high, low)
    lane = lax.broadcasted_iota(jnp.int32, (48, 128), 1)
    sub = jnp.where(lane < SUBC, low[:48], pltpu.roll(low[48:], SUBC, 1))
    for k in range(8):
        sub_ref[k] = sub


def first_kernel(wait, ins, outs, scratch):
    jac_ref, mat_ref, geo_ref, stiff_ref, state_ref = ins
    ejac_ref, p_ref, outer_ref, inner_ref, sub_ref = outs
    k_ref, y_ref, matrix_ref = scratch
    wait(0)
    for m in range(3):
        for v in range(V):
            for c in range(3):
                matrix_ref[m * 3 + c, v : v + 1, :] = jac_ref[m, v, c : c + 1, :]
    wait(1, 2)
    material = mat_ref[...]
    for w in range(V):
        parts = [
            by_material(material, lambda m: matrix_ref[m * 3 + c, :, w : w + 1])
            for c in range(3)
        ]
        for i in range(3):
            row = (i * V + w) * V
            ejac_ref[row : row + V, :] = (
                geo_ref[i, 0:1, :] * parts[0]
                + geo_ref[i, 1:2, :] * parts[1]
                + geo_ref[i, 2:3, :] * parts[2]
            )
    wait(3, 4)
    padded_stiffness(stiff_ref, k_ref)
    values = [state_ref[v] for v in range(V)]
    matrix = k_ref[...]
    one = star(values, matrix, ejac_ref, y_ref)
    two = star(one, matrix, ejac_ref, y_ref)
    out = [
        DT * state_ref[v] - DT**2 / 2 * one[v] + DT**3 / 6 * two[v] for v in range(V)
    ]
    pack(out, p_ref, outer_ref, inner_ref, sub_ref)


def split(values):
    high = values.astype(bf16)
    low = (values - high.astype(f32)).astype(bf16)
    return jnp.concatenate([high, low], axis=0)


def one_hot(index, start, count):
    places = lax.broadcasted_iota(jnp.int32, (count, E), 0) + start
    return jnp.where(places == index, 1.0, 0.0).astype(bf16)


def gathered(pieces, picks, n_ref):
    for face in range(4):
        both = jnp.dot(pieces, picks(face), preferred_element_type=f32)
        n_ref[:, face * E : (face + 1) * E] = both[:ROWS] + both[ROWS:]


def neighbour_flux(n_ref, turn_ref, minus_ref, total):
    for face in range(4):
        lanes = slice(face * E, (face + 1) * E)
        if face == 0:
            across = [None] * V
        for b in range(B):
            turn = turn_ref[face * B + b]
            for w in range(V):
                row = row_of(w, b)
                term = turn * n_ref[row : row + 1, lanes]
                across[w] = term if across[w] is None else across[w] + term
    for w in range(V):
        mixed(total, minus_ref, w, across[w])
    return total


def unpacked(p_ref, v):
    tail = 72 + 2 * v
    return jnp.concatenate([p_ref[8 * v : 8 * v + 8, :], p_ref[tail : tail + 2, :]], axis=0)


def local_part(p_ref, matrix_ref, near_ref, scale_ref, ejac_ref, plus_ref, minus_ref,
               turn_ref, y_ref, n_ref, out_ref):
    picks = lambda face: one_hot(near_ref[face : face + 1, :], 0, E)
    mapped(matrix_ref[...], [unpacked(p_ref, v) for v in range(V)], y_ref)
    gathered(split(p_ref[...]), picks, n_ref)
    total = [None] * V
    for i in range(3):
        for w in range(V):
            mixed(total, ejac_ref, i * V + w, block(y_ref, i, w))
    for v in range(V):
        out_ref[v] = total[v]
    total = [None] * V
    for w in range(V):
        own = scale_ref[0:1, :] * block(y_ref, 3, w)
        for face in range(1, 4):
            own = own + scale_ref[face : face + 1, :] * block(y_ref, 3 + face, w)
        mixed(total, plus_ref, w, own)
    for v in range(V):
        out_ref[v] = out_ref[v] - total[v]
    total = neighbour_flux(n_ref, turn_ref, minus_ref, [None] * V)
    for v in range(V):
        out_ref[v] = out_ref[v] - total[v]


def local_kernel_one(wait, ins, outs, scratch):
    (fneigh_ref, orient_ref, scale_ref, fplus_ref, fminus_ref, mat_ref, stiff_ref,
     flocal_ref, near_ref, p_ref, ejac_ref) = ins
    out_ref, plus_ref, minus_ref, turn_ref, matrix_ref = outs
    y_ref, n_ref, rows_plus, rows_minus, rows_neigh, k_ref = scratch
    wait(0, 1, 2)
    by_matrix(fneigh_ref, rows_neigh)
    for face in range(4):
        way = orient_ref[face : face + 1, :]
        scale = scale_ref[face : face + 1, :]
        masks = [jnp.broadcast_to(way == t, (B, E)) for t in range(11)]
        for b in range(B):
            chosen = jnp.broadcast_to(rows_neigh[11, :, b : b + 1], (B, E))
            for t in range(11):
                column = jnp.broadcast_to(rows_neigh[t, :, b : b + 1], (B, E))
                chosen = jnp.where(masks[t], column, chosen)
            turn_ref[face * B + b] = chosen * scale
    wait(3, 4, 5)
    material = mat_ref[...]
    by_matrix(fplus_ref, rows_plus)
    by_matrix(fminus_ref, rows_minus)
    for w in range(V):
        rows = slice(w * V, w * V + V)
        plus_ref[rows, :] = by_material(material, lambda m: rows_plus[m, :, w : w + 1])
        minus_ref[rows, :] = by_material(material, lambda m: rows_minus[m, :, w : w + 1])
    wait(6, 7)
    padded_stiffness(stiff_ref, k_ref)
    matrix_ref[...] = jnp.zeros_like(matrix_ref)
    for i in range(3):
        matrix_ref[16 * i : 16 * i + B, :] = k_ref[16 * i : 16 * i + B, :].T
    for a in range(B):
        for face in range(4):
            row = 48 + 16 * face + a
            matrix_ref[row : row + 1, :] = flocal_ref[a, face : face + 1, :]
    wait(8, 9, 10)
    local_part(p_ref, matrix_ref, near_ref, scale_ref, ejac_ref, plus_ref, minus_ref,
               turn_ref, y_ref, n_ref, out_ref)


def local_kernel_two(wait, ins, outs, scratch):
    p_ref, matrix_ref, near_ref, ejac_ref, scale_ref, plus_ref, turn_ref, minus_ref = ins
    wait(*range(8))
    local_part(p_ref, matrix_ref, near_ref, scale_ref, ejac_ref, plus_ref, minus_ref,
               turn_ref, *scratch, *outs)


def remote_flux(wait, ins, n_ref):
    near_ref, outer_ref, inner_ref, group_ref, turn_ref, minus_ref = ins
    even = is_even()

    def picks(face):
        index = near_ref[face : face + 1, :]
        swapped = jnp.where(index >= 768, index ^ 128, index)
        return one_hot(jnp.where(even, index, swapped), E, 768)

    wait(0, 1, 2, 3)
    lane = lax.broadcasted_iota(jnp.int32, (48, 128), 1)
    table = []
    for pair in range(4):
        one = group_ref[2 * pair]
        two = group_ref[2 * pair + 1]
        top = jnp.where(lane < SUBC, one, pltpu.roll(two, SUBC, 1))
        bottom = jnp.where(lane < SUBC, pltpu.roll(one, SUBC, 1), two)
        table.append(jnp.concatenate([top, bottom], axis=0))
    table += [outer_ref[...], inner_ref[...]]
    gathered(split(jnp.concatenate(table, axis=1)), picks, n_ref)
    wait(4, 5)
    return neighbour_flux(n_ref, turn_ref, minus_ref, [None] * V)


def middle_kernel(wait, ins, outs, scratch):
    state_ref, local_ref, cluster_ref, ejac_ref, stiff_ref = ins[6:]
    base_ref, p_ref, outer_ref, inner_ref, sub_ref = outs
    n_ref, k_ref, y_ref, m_ref = scratch
    flux = remote_flux(wait, ins[:6], n_ref)
    wait(6, 7, 8)
    coarse = cluster_ref[...].astype(f32)
    fine = 1.0 - coarse
    for v in range(V):
        change = local_ref[v] - flux[v]
        base_ref[v] = state_ref[v] + change
        m_ref[v] = state_ref[v] + fine * change
    wait(9, 10)
    padded_stiffness(stiff_ref, k_ref)
    matrix = k_ref[...]
    one = star([m_ref[v] for v in range(V)], matrix, ejac_ref, y_ref)
    two = star(one, matrix, ejac_ref, y_ref)
    weight_one = DT**2 / 2 + DT**2 * coarse
    weight_two = DT**3 / 6 + DT**3 * coarse
    out = [
        DT * m_ref[v] - weight_one * one[v] + weight_two * two[v] for v in range(V)
    ]
    pack(out, p_ref, outer_ref, inner_ref, sub_ref)


def last_kernel(wait, ins, outs, scratch):
    base_ref, local_ref = ins[6:]
    flux = remote_flux(wait, ins[:6], *scratch)
    wait(6, 7)
    for v in range(V):
        outs[0][v] = base_ref[v] + (local_ref[v] - flux[v])


def arr(*shape, dtype=f32):
    return jax.ShapeDtypeStruct(shape, dtype)


def call(kernel, outs, scratch, flops, *operands):
    count = len(operands)

    def body(*refs):
        given, rest = refs[:count], refs[count:]
        results, rest = rest[: len(outs)], rest[len(outs) :]
        held, rest = rest[:count], rest[count:]
        copies = [
            pltpu.make_async_copy(given[i], held[i], rest[-1].at[i]) for i in range(count)
        ]
        for copy in copies:
            copy.start()

        def wait(*which):
            for i in which:
                copies[i].wait()

        kernel(wait, held, results, rest[:-1])

    return pl.pallas_call(
        body,
        out_shape=outs,
        in_specs=[pl.BlockSpec(memory_space=pltpu.HBM)] * count,
        scratch_shapes=[pltpu.VMEM(x.shape, x.dtype) for x in operands]
        + [pltpu.VMEM(shape, f32) for shape in scratch]
        + [pltpu.SemaphoreType.DMA((count,))],
        compiler_params=pltpu.CompilerParams(vmem_limit_bytes=67043328),
        cost_estimate=pl.CostEstimate(flops=flops, bytes_accessed=1 << 20, transcendentals=0),
    )(*operands)


def swapped_pairs(size, offset):
    route = []
    for i in range(offset, size + offset, 2):
        one, two = i % size, (i + 1) % size
        route += [(one, two), (two, one)]
    return route


def exchange(outer, inner, sub):
    size = lax.axis_size("dom")
    outer = lax.ppermute(outer, "dom", swapped_pairs(size, 1))
    inner = lax.ppermute(inner, "dom", swapped_pairs(size, 0))
    group = lax.all_to_all(sub, "sub", 0, 0, tiled=True)
    return group, outer, inner


def shards(state, geometry, face_scale, material, cluster, neighbours, orientation,
           stiffness, jacobians, flux_local, flux_neigh, flux_plus, flux_minus):
    material = material.reshape(1, E)
    cluster = cluster.reshape(1, E)
    cube = arr(V, B, E)
    square = arr(V * V, E)
    packed = [arr(ROWS, E), arr(ROWS, COPY), arr(ROWS, COPY), arr(8, 48, 128)]
    wide = (112, V * E)
    narrow = (48, V * E)
    picked = (ROWS, 4 * E)
    jac, stiff, flocal, fneigh, fplus, fminus = [
        jnp.transpose(x, order)
        for x, order in [(jacobians, (0, 2, 1, 3))]
        + [(x, (1, 0, 2)) for x in (stiffness, flux_local, flux_neigh, flux_plus, flux_minus)]
    ]

    ejac, p, outer, inner, sub = call(
        first_kernel, [arr(27 * V, E), *packed], [(48, B), narrow, (V, V, V)],
        1 << 28, jac, material, geometry, stiff, state,
    )
    group, outer, inner = exchange(outer, inner, sub)
    local, plus, minus, turn, matrix = call(
        local_kernel_one,
        [cube, square, square, arr(4 * B, B, E), arr(112, B)],
        [wide, picked, (3, V, V), (3, V, V), (12, B, B), (48, B)], 1 << 33,
        fneigh, orientation, face_scale, fplus, fminus, material, stiff, flocal,
        neighbours, p, ejac,
    )
    base, p, outer, inner, sub = call(
        middle_kernel, [cube, *packed], [picked, (48, B), narrow, (V, B, E)],
        1 << 28, neighbours, outer, inner, group, turn, minus,
        state, local, cluster, ejac, stiff,
    )
    group, outer, inner = exchange(outer, inner, sub)
    local, = call(
        local_kernel_two, [cube], [wide, picked], 1 << 33,
        p, matrix, neighbours, ejac, face_scale, plus, turn, minus,
    )
    return call(
        last_kernel, [cube], [picked], 1 << 28,
        neighbours, outer, inner, group, turn, minus, base, local,
    )[0]


def solution(mesh):
    whole = ("dom", "sub")
    placed = (
        P(None, None, whole), P(None, None, whole), P(None, whole), P(whole), P(whole),
        P(None, whole), P(None, whole), P(), P(), P(), P(), P(), P(),
    )
    return jax.shard_map(
        shards, mesh=mesh, in_specs=placed, out_specs=P(None, None, whole), check_vma=False
    )
```

time: 68.9 us -> 55 us (0.80)
  the two profiles are of different devices: /device:TPU:8 before, /device:TPU:2 now
where the time goes in v2:
time: 55 us; the launch traced here: 54.5 us
  starting transfers between devices  34.5 us (63%)
  Pallas kernels  17.8 us (32%)
  waiting for transfers between devices  2.12 us (4%)
    all_to_all x2, starting transfers between devices, exchange(): group = lax.all_to_all(sub, 'sub', 0, 0, tiled=True)  19.2 us
    pallas_call x5, Pallas kernels, call(): pl.pallas_call(body, out_shape=outs, in_specs=[pl.BlockSpec(memory_space=...  17.8 us
    ppermute x2, starting transfers between devices, exchange(): outer = lax.ppermute(outer, 'dom', swapped_pairs(size, 1))  11.5 us
    ppermute x2, starting transfers between devices, exchange(): inner = lax.ppermute(inner, 'dom', swapped_pairs(size, 0))  3.84 us
    ppermute x2, waiting for transfers between devices, exchange(): outer = lax.ppermute(outer, 'dom', swapped_pairs(size, 1))  2.11 us
  transfers between devices with their start and end apart: 6, of which 1 were waited for; matrix products, arithmetic and copies ran while one was open for 0% of the time, Pallas kernels for 15%

profile of v2, /device:TPU:2, one launch (start us, length us, event | category | flops | bytes accessed | tf_op | source)
XLA Modules:
  0.0 54.5 jit_solution(14862960950599280095)
XLA Ops:
  0.0 3.0 %shard_map.127 = (f32[243,256]{1,0:T(8,128)}, f32[96,256]{1,0:T(8,128)}, f32[96,128]{1,0:T(8,128)}, f32[96,128]{1,0:T(8,128)}, f32[8,48,128]{2,1,0:T(8,128)}) custom-call(f32[3,9,3,9]{3,2,1,0:T(4,128)} %bitcast.13, s32[1,256]{1,0:T(1,128)} %bitcast.17, f32[3,3,256]{2,1,0:T(4,128)} %refs_2_.3, f32[10,3,10]{2,1,0:T(4,128)} %bitcast.8, f32[9,10,256]{2,1,0:T(8,128)} %refs_6_.1), custom_call_target="tpu_custom_call" | custom-call | flops 268435456 | bytes 1048576 | tf_op jit(solution)/shard_map/pallas_call | solution.py:312
  3.0 13.4 %all-to-all-start = ((f32[8,48,128]{2,1,0:T(8,128)}), f32[8,48,128]{2,1,0:T(8,128)}, u32[]{:S(2)}, u32[]{:S(2)}) async-start(f32[8,48,128]{2,1,0:T(8,128)} %get-tuple-element.22), calls=%async_computation | async-start | bytes 393216 | tf_op jit(solution)/shard_map/all_to_all | solution.py:336
  16.4 8.7 %collective-permute-start = (f32[96,128]{1,0:T(8,128)}, f32[96,128]{1,0:T(8,128)}, u32[]{:S(2)}, u32[]{:S(2)}) collective-permute-start(f32[96,128]{1,0:T(8,128)} %get-tuple-element.20), channel_id=1, source_target_pairs={{8,16},{16,8},{24,32},{32,24},{40,48},{48,40},{56,64},{64,56},{72,... | collective-permute-start | bytes 147464 | tf_op jit(solution)/shard_map/ppermute | solution.py:334
  25.1 1.9 %collective-permute-start.1 = (f32[96,128]{1,0:T(8,128)}, f32[96,128]{1,0:T(8,128)}, u32[]{:S(2)}, u32[]{:S(2)}) collective-permute-start(f32[96,128]{1,0:T(8,128)} %get-tuple-element.21), channel_id=1, source_target_pairs={{0,8},{8,0},{16,24},{24,16},{32,40},{40,32},{48,56},{56,48},{64,72... | collective-permute-start | bytes 147464 | tf_op jit(solution)/shard_map/ppermute | solution.py:335
  27.0 4.6 %shard_map.128 = (f32[9,10,256]{2,1,0:T(8,128)}, f32[81,256]{1,0:T(8,128)}, f32[81,256]{1,0:T(8,128)}, f32[40,10,256]{2,1,0:T(8,128)}, f32[112,10]{1,0:T(8,128)}) custom-call(f32[10,12,10]{2,1,0:T(8,128)} %bitcast.12, s32[4,256]{1,0:T(4,128)} %refs_1_.1, f32[4,256]{1,0:T(4,128)} %refs_4_.3, f32[9,3,9]{2,1,0:T(4,128)} %bitcast.15, f32[9,3,9]{2,1,0:T(4,128)} %bitcast.16, ...), custom_call_target="tpu_custom_call" | custom-call | flops 8589934592 | bytes 1048576 | tf_op jit(solution)/shard_map/pallas_call | solution.py:312
  31.6 0.0 collective-permute-done.refs_1_
  31.6 0.0 collective-permute-done.1.refs_2_
  31.6 0.0 all-to-all-done.refs_3_
  31.7 3.9 %shard_map.129 = (f32[9,10,256]{2,1,0:T(8,128)}, f32[96,256]{1,0:T(8,128)}, f32[96,128]{1,0:T(8,128)}, f32[96,128]{1,0:T(8,128)}, f32[8,48,128]{2,1,0:T(8,128)}) custom-call(s32[4,256]{1,0:T(4,128)} %refs_0_.3, f32[96,128]{1,0:T(8,128)} %collective-permute-done.refs_1_, f32[96,128]{1,0:T(8,128)} %collective-permute-done.1.refs_2_, ...), custom_call_target="tpu_custom_call" | custom-call | flops 268435456 | bytes 1048576 | tf_op jit(solution)/shard_map/pallas_call | solution.py:312
  35.6 5.7 %all-to-all-start.1 = ((f32[8,48,128]{2,1,0:T(8,128)}), f32[8,48,128]{2,1,0:T(8,128)}, u32[]{:S(2)}, u32[]{:S(2)}) async-start(f32[8,48,128]{2,1,0:T(8,128)} %get-tuple-element.30), calls=%async_computation.1 | async-start | bytes 393216 | tf_op jit(solution)/shard_map/all_to_all | solution.py:336
  41.3 2.8 %collective-permute-start.2 = (f32[96,128]{1,0:T(8,128)}, f32[96,128]{1,0:T(8,128)}, u32[]{:S(2)}, u32[]{:S(2)}) collective-permute-start(f32[96,128]{1,0:T(8,128)} %get-tuple-element.28), channel_id=1, source_target_pairs={{8,16},{16,8},{24,32},{32,24},{40,48},{48,40},{56,64},{64,56},{72,... | collective-permute-start | bytes 147464 | tf_op jit(solution)/shard_map/ppermute | solution.py:334
  44.1 1.9 %collective-permute-start.3 = (f32[96,128]{1,0:T(8,128)}, f32[96,128]{1,0:T(8,128)}, u32[]{:S(2)}, u32[]{:S(2)}) collective-permute-start(f32[96,128]{1,0:T(8,128)} %get-tuple-element.29), channel_id=1, source_target_pairs={{0,8},{8,0},{16,24},{24,16},{32,40},{40,32},{48,56},{56,48},{64,72... | collective-permute-start | bytes 147464 | tf_op jit(solution)/shard_map/ppermute | solution.py:335
  46.0 3.6 %shard_map.130.refs_7_ = f32[9,10,256]{2,1,0:T(8,128)} custom-call(f32[96,256]{1,0:T(8,128)} %get-tuple-element.32.refs_0_, f32[112,10]{1,0:T(8,128)} %get-tuple-element.33.refs_1_, s32[4,256]{1,0:T(4,128)} %refs_0_.3, f32[243,256]{1,0:T(8,128)} %get-tuple-element.24.refs_10_.refs_9_.refs_3_, f32[4,256]{1,0:T(4,128)} %refs_4_.3, ...), custom_call_target="tpu_custom_call" | custom-call | flops 8589934592 | bytes 1048576 | tf_op jit(solution)/shard_map/pallas_call | solution.py:312
  49.6 2.1 %collective-permute-done.2.refs_1_ = f32[96,128]{1,0:T(8,128)} collective-permute-done((f32[96,128]{1,0:T(8,128)}, f32[96,128]{1,0:T(8,128)}, u32[]{:S(2)}, u32[]{:S(2)}) %collective-permute-start.2) | collective-permute-done | bytes 49184 | tf_op jit(solution)/shard_map/ppermute | solution.py:334
  51.7 0.0 collective-permute-done.3.refs_2_
  51.7 0.0 all-to-all-done.1.refs_3_
  51.7 2.7 %shard_map.131 = f32[9,10,256]{2,1,0:T(8,128)} custom-call(s32[4,256]{1,0:T(4,128)} %refs_0_.3, f32[96,128]{1,0:T(8,128)} %collective-permute-done.2.refs_1_, f32[96,128]{1,0:T(8,128)} %collective-permute-done.3.refs_2_, f32[8,48,128]{2,1,0:T(8,128)} %all-to-all-done.1.refs_3_, f32[40,10,256]{2,1,0:T(8,128)} %get-tuple-element.25.refs_4_.refs_6_, ...), custom_call_target="tpu_custom_call" | custom-call | flops 268435456 | bytes 1048576 | tf_op jit(solution)/shard_map/pallas_call | solution.py:312
Async XLA Ops:
  3.0 28.7 %all-to-all-start = ((f32[8,48,128]{2,1,0:T(8,128)}), f32[8,48,128]{2,1,0:T(8,128)}, u32[]{:S(2)}, u32[]{:S(2)}) async-start(f32[8,48,128]{2,1,0:T(8,128)} %get-tuple-element.22), calls=%async_computation | async-start | bytes 393216 | tf_op jit(solution)/shard_map/all_to_all | solution.py:336
  16.4 15.2 %collective-permute-start = (f32[96,128]{1,0:T(8,128)}, f32[96,128]{1,0:T(8,128)}, u32[]{:S(2)}, u32[]{:S(2)}) collective-permute-start(f32[96,128]{1,0:T(8,128)} %get-tuple-element.20), channel_id=1, source_target_pairs={{8,16},{16,8},{24,32},{32,24},{40,48},{48,40},{56,64},{64,56},{72,... | collective-permute-start | bytes 147464 | tf_op jit(solution)/shard_map/ppermute | solution.py:334
  25.1 6.6 %collective-permute-start.1 = (f32[96,128]{1,0:T(8,128)}, f32[96,128]{1,0:T(8,128)}, u32[]{:S(2)}, u32[]{:S(2)}) collective-permute-start(f32[96,128]{1,0:T(8,128)} %get-tuple-element.21), channel_id=1, source_target_pairs={{0,8},{8,0},{16,24},{24,16},{32,40},{40,32},{48,56},{56,48},{64,72... | collective-permute-start | bytes 147464 | tf_op jit(solution)/shard_map/ppermute | solution.py:335
  35.6 16.2 %all-to-all-start.1 = ((f32[8,48,128]{2,1,0:T(8,128)}), f32[8,48,128]{2,1,0:T(8,128)}, u32[]{:S(2)}, u32[]{:S(2)}) async-start(f32[8,48,128]{2,1,0:T(8,128)} %get-tuple-element.30), calls=%async_computation.1 | async-start | bytes 393216 | tf_op jit(solution)/shard_map/all_to_all | solution.py:336
  41.3 10.5 %collective-permute-start.2 = (f32[96,128]{1,0:T(8,128)}, f32[96,128]{1,0:T(8,128)}, u32[]{:S(2)}, u32[]{:S(2)}) collective-permute-start(f32[96,128]{1,0:T(8,128)} %get-tuple-element.28), channel_id=1, source_target_pairs={{8,16},{16,8},{24,32},{32,24},{40,48},{48,40},{56,64},{64,56},{72,... | collective-permute-start | bytes 147464 | tf_op jit(solution)/shard_map/ppermute | solution.py:334
  44.1 7.7 %collective-permute-start.3 = (f32[96,128]{1,0:T(8,128)}, f32[96,128]{1,0:T(8,128)}, u32[]{:S(2)}, u32[]{:S(2)}) collective-permute-start(f32[96,128]{1,0:T(8,128)} %get-tuple-element.29), channel_id=1, source_target_pairs={{0,8},{8,0},{16,24},{24,16},{32,40},{40,32},{48,56},{56,48},{64,72... | collective-permute-start | bytes 147464 | tf_op jit(solution)/shard_map/ppermute | solution.py:335
